TPU v7x, 256 devices: a whole 4x4x8 slice. The times are simulated.
256 devices in a mesh: seq: 32 (over x_lo, z, core), head: 8 (over y, x_hi).
Axes of the slice: x: 4 (x_hi: 2, x_lo: 2; x = x_hi * 2 + x_lo), y: 4, z: 8, core: 2. Of those that a mesh axis runs over, the one named last changes fastest.
Arguments:
- query_rows: bfloat16 [6144, 2048], P('seq', 'head'), may hold values from -6 to 6
- key_rows: bfloat16 [6144, 2048], P('seq', 'head'), may hold values from -6 to 6
- value_rows: bfloat16 [6144, 2048], P('seq', 'head'), may hold values from -6 to 6
- grad_output: bfloat16 [6144, 2048], P('seq', 'head'), may hold values from -6 to 6
- positions: int32 [6144], P('seq'), may hold values from 0 to 6143, each once
Outputs:
- grad_query: bfloat16 [6144, 2048], P(('seq', 'head'))
- grad_keys: bfloat16 [6144, 2048], P('seq', 'head')
- grad_values: bfloat16 [6144, 2048], P('seq', 'head')
Inputs may be any that keep to these rules, and one draw needn't show every extreme that they name: `positions`: each number from 0 to 6143 appears once.
All inputs are finite; a program needn't handle non-finite values.
Results may differ from a plain program's by a relative error of at most 0.012.
Values may be sent and summed in bfloat16 or wider, within the bound.
No kernel may reach another device: no remote copies, remote signals or barrier semaphores. Data moves between devices by JAX's collectives and lax.ppermute only.
A program may use at most 128 MiB of HBM per device.

v0:
```python
import functools

import jax
import jax.numpy as jnp
from jax import lax
from jax.experimental import pallas as pl
from jax.experimental.pallas import tpu as pltpu
from jax.sharding import PartitionSpec as P

HEAD_DIM = 128
ROWS = 192
BOTH = 2 * ROWS
QUAD = 4
QUERIES = QUAD * BOTH
HALF_KEYS = 2 * BOTH
TILE = 256
FIRST_MIB = 16
GRADS_MIB = 16
LOG2E = 1.4426950408889634
SCALE = HEAD_DIM**-0.5
LOW = -1e30
F32 = jnp.float32
BF16 = jnp.bfloat16


def z_of(j, half):
    return 2 * j + half


def perm(xor_x=0, xor_j=0, xor_half=0, xor_core=0):
    pairs = []
    for x in range(2):
        for j in range(4):
            for h in range(2):
                for c in range(2):
                    src = x * 16 + z_of(j, h) * 2 + c
                    dst = (x ^ xor_x) * 16 + z_of(j ^ xor_j, h ^ xor_half) * 2 + (c ^ xor_core)
                    pairs.append((src, dst))
    return pairs


def move(value, **how):
    return lax.ppermute(value, "seq", perm(**how))


def near_move(value, t):
    return move(value, xor_x=t // 2, xor_half=t % 2)


def pack(first, second, positions):
    high = (positions // 128).astype(BF16)
    low = (positions % 128).astype(BF16)
    tags = jnp.stack([high, low])
    tags = jnp.pad(tags, ((0, 0), (0, 2 * HEAD_DIM - ROWS)))
    tags = jnp.broadcast_to(tags[:, None, :], (2, 8, 2 * HEAD_DIM)).reshape(16, 2 * HEAD_DIM)
    return jnp.concatenate([first, second, tags], axis=0)


def places(packed_ref):
    tags = packed_ref[BOTH : BOTH + 16, :].astype(F32)
    return tags[0:8] * 128.0 + tags[8:16]


def split(packed_ref, cols, first, second, start):
    first[pl.ds(start, ROWS), :] = packed_ref[0:ROWS, cols]
    second[pl.ds(start, ROWS), :] = packed_ref[ROWS:BOTH, cols]


def head_cols(core):
    return pl.ds(pl.multiple_of(core * HEAD_DIM, HEAD_DIM), HEAD_DIM)


def take_queries(where_ref, refs, queries, grads, query_pos):
    mine, core = where_ref[0], where_ref[1]
    lane = lax.broadcasted_iota(jnp.int32, (8, 128), 1)
    for t in range(QUAD):
        chip = (mine ^ t) * BOTH
        for far in range(2):
            start = pl.multiple_of(chip + (core ^ far) * ROWS, 64)
            split(refs[2 * t + far], head_cols(core), queries, grads, start)
        own, other = places(refs[2 * t]), places(refs[2 * t + 1])
        left = jnp.where(core == 0, own, other)
        right = jnp.where(core == 0, other, own)
        turned_a = pltpu.roll(right[:, 0:128], 64, 1)
        turned_b = pltpu.roll(right[:, 128:256], 64, 1)
        row = jnp.concatenate(
            [left[:, 0:128], jnp.where(lane < 64, left[:, 128:256], turned_a), jnp.where(lane < 64, turned_a, turned_b)],
            axis=1,
        )
        query_pos[:, pl.ds(pl.multiple_of(chip, 128), BOTH)] = row


def take_keys(where_ref, refs, keys, values, key_pos):
    core = where_ref[1]
    for n in range(4):
        start = pl.multiple_of((n // 2) * BOTH + (core ^ (n % 2)) * ROWS, 64)
        split(refs[n], head_cols(core), keys, values, start)
        tall = jnp.concatenate([places(refs[n])] * 16, axis=0)
        key_pos[pl.ds(start, 128), :] = jnp.transpose(tall[:, 0:128])
        key_pos[pl.ds(start + 128, 64), :] = jnp.transpose(tall[:, 128:256])[0:64]


def dot_t(a, b):
    return lax.dot_general(a, b, (((1,), (1,)), ((), ())), preferred_element_type=F32)


def masked_scores(queries, keys, query_pos, key_pos, start):
    s = dot_t(keys[pl.ds(start, TILE), :], queries[...])
    s = s.reshape(TILE // 8, 8, QUERIES) * (SCALE * LOG2E)
    place = key_pos[pl.ds(start, TILE), :].reshape(TILE // 8, 8, 128)
    place = jnp.concatenate([place] * (QUERIES // 128), axis=2)
    return jnp.where(place <= query_pos[...][None], s, LOW)


def sweep(queries, grads, query_pos, keys, values, key_pos, scores, products, running):
    def turn(i, running):
        top, total, delta = running
        start = pl.multiple_of(i * TILE, TILE)
        s = masked_scores(queries, keys, query_pos, key_pos, start)
        g = dot_t(values[pl.ds(start, TILE), :], grads[...])
        scores[pl.ds(start, TILE), :] = s.reshape(TILE, QUERIES)
        products[pl.ds(start, TILE), :] = g
        g = g.reshape(TILE // 8, 8, QUERIES)
        new = jnp.maximum(top, jnp.max(s, axis=0))
        shrink = jnp.exp2(top - new)
        p = jnp.exp2(s - new[None])
        total = total * shrink + jnp.sum(p, axis=0)
        delta = delta * shrink + jnp.sum(p * g, axis=0)
        return new, total, delta

    return lax.fori_loop(0, HALF_KEYS // TILE, turn, running)


def first_kernel(where_ref, *refs):
    query_refs, key_refs = refs[0:8], refs[8:12]
    queries, grads, query_pos, keys, scores, products, out, values, key_pos = refs[12:]
    take_queries(where_ref, query_refs, queries, grads, query_pos)
    take_keys(where_ref, key_refs, keys, values, key_pos)
    start = (
        jnp.full((8, QUERIES), LOW, F32),
        jnp.zeros((8, QUERIES), F32),
        jnp.zeros((8, QUERIES), F32),
    )
    found = sweep(queries, grads, query_pos, keys, values, key_pos, scores, products, start)
    for n in range(3):
        out[n] = found[n]


def second_kernel(where_ref, *refs):
    queries, grads, query_pos, before = refs[0:4]
    key_refs = refs[4:8]
    keys, scores, products, out, values, key_pos = refs[8:]
    take_keys(where_ref, key_refs, keys, values, key_pos)
    running = (before[0], before[1], before[2])
    top, total, delta = sweep(queries, grads, query_pos, keys, values, key_pos, scores, products, running)
    best = jnp.max(top, axis=0, keepdims=True)
    shrink = jnp.exp2(top - best)
    out[0:1, :] = best
    out[1:2, :] = jnp.sum(total * shrink, axis=0, keepdims=True)
    out[2:3, :] = jnp.sum(delta * shrink, axis=0, keepdims=True)
    out[3:8, :] = jnp.zeros((5, QUERIES), F32)


def grads_kernel(where_ref, *refs):
    queries, grads = refs[0:2]
    key_refs = refs[2:8]
    stat_refs = refs[8:12]
    own_query, query_outs = refs[12], refs[13:16]
    own_keys, key_outs = refs[16], refs[17:20]
    query_sum, query_rows = refs[20:]
    mine = where_ref[0]
    stats = [r[...] for r in stat_refs]
    tops = [s[0:1] for s in stats]
    best = functools.reduce(jnp.maximum, tops)
    shrinks = [jnp.exp2(t - best) for t in tops]
    total = sum(s[1:2] * w for s, w in zip(stats, shrinks))
    delta = sum(s[2:3] * w for s, w in zip(stats, shrinks)) / total
    log_total = jnp.broadcast_to(best + jnp.log2(total), (8, QUERIES))
    delta = jnp.broadcast_to(delta, (8, QUERIES))
    query_sum[...] = jnp.zeros_like(query_sum)
    for part in range(2):
        keys, scores, products = key_refs[3 * part : 3 * part + 3]
        for n in range(HALF_KEYS // TILE):
            start = n * TILE
            s = scores[start : start + TILE, :].reshape(TILE // 8, 8, QUERIES)
            g = products[start : start + TILE, :].reshape(TILE // 8, 8, QUERIES)
            p = jnp.exp2(s - log_total[None])
            d = (p * (g - delta[None])).reshape(TILE, QUERIES).astype(BF16)
            p = p.reshape(TILE, QUERIES).astype(BF16)
            grad_value = jnp.dot(p, grads[...], preferred_element_type=F32)
            grad_key = jnp.dot(d, queries[...], preferred_element_type=F32) * SCALE
            keys_t = jnp.transpose(keys[start : start + TILE, :])
            query_sum[...] += jnp.dot(keys_t, d, preferred_element_type=F32)
            at = 0
            while at < TILE:
                row = start + at
                chunk, inside = 2 * part + row // BOTH, row % BOTH
                size = min(TILE - at, BOTH - inside)
                target = own_keys if chunk == 0 else key_outs[chunk - 1]
                target[inside : inside + size, :] = grad_key[at : at + size].astype(target.dtype)
                target[BOTH + inside : BOTH + inside + size, :] = grad_value[at : at + size].astype(target.dtype)
                at += size
    query_rows[...] = jnp.transpose(query_sum[...]) * SCALE
    for t in range(QUAD):
        rows = query_rows[pl.ds(pl.multiple_of((mine ^ t) * BOTH, BOTH), BOTH), :]
        if t == 0:
            own_query[...] = rows
        else:
            query_outs[t - 1][...] = rows.astype(BF16)


def in_vmem(n):
    return [pl.BlockSpec(memory_space=pltpu.VMEM)] * n


def shaped(*shape, dtype=BF16):
    return jax.ShapeDtypeStruct(shape, dtype)


def call(kernel, outs, scratch, flops, mib, where, *args):
    return pl.pallas_call(
        kernel,
        out_shape=tuple(outs),
        in_specs=[pl.BlockSpec(memory_space=pltpu.SMEM)] + in_vmem(len(args)),
        out_specs=tuple(in_vmem(len(outs))),
        scratch_shapes=scratch,
        compiler_params=pltpu.CompilerParams(vmem_limit_bytes=mib * 1024 * 1024),
        cost_estimate=pl.CostEstimate(flops=flops, bytes_accessed=4 * 10**6, transcendentals=0),
    )(where, *args)


def heads_of_own_rows(value, core):
    kept = lax.dynamic_index_in_dim(value, core, 0, False)
    sent = lax.dynamic_index_in_dim(value, 1 - core, 0, False)
    came = move(sent, xor_core=1)
    first = jnp.where(core == 0, kept, came)
    last = jnp.where(core == 0, came, kept)
    return jnp.concatenate([first, last], axis=-1)


def body(query_rows, key_rows, value_rows, grad_output, positions):
    place = lax.axis_index("seq")
    core = place % 2
    where = jnp.stack([(place // 16) * 2 + (place // 2) % 2, core]).astype(jnp.int32)
    key_pack = pack(key_rows, value_rows, positions)
    query_pack = pack(query_rows, grad_output, positions)
    key_packs = [key_pack] + [move(key_pack, xor_j=t) for t in range(1, 4)]
    query_z = move(query_pack, xor_half=1)
    query_x = move(query_pack, xor_x=1)
    query_packs = [query_pack, query_z, query_x, move(query_z, xor_x=1)]
    all_keys = [v for k in key_packs for v in (k, move(k, xor_core=1))]
    all_queries = [v for q in query_packs for v in (q, move(q, xor_core=1))]

    rows = [shaped(QUERIES, 128), shaped(QUERIES, 128), shaped(8, QUERIES, dtype=F32)]
    tall = shaped(HALF_KEYS, QUERIES, dtype=F32)
    half = [shaped(HALF_KEYS, 128), tall, tall]
    spare = [pltpu.VMEM((HALF_KEYS, 128), BF16), pltpu.VMEM((HALF_KEYS, 128), F32)]
    *taken, keys_a, scores_a, products_a, running = call(
        first_kernel, rows + half + [shaped(3, 8, QUERIES, dtype=F32)], spare, 2 * 10**9, FIRST_MIB, where,
        *all_queries, *all_keys[:4],
    )
    keys_b, scores_b, products_b, stats = call(
        second_kernel, half + [shaped(8, QUERIES, dtype=F32)], spare, 2 * 10**9, FIRST_MIB, where,
        *taken, running, *all_keys[4:],
    )
    all_stats = [stats] + [near_move(stats, t) for t in range(1, QUAD)]
    outs = call(
        grads_kernel,
        [shaped(BOTH, 128, dtype=F32)] + [shaped(BOTH, 128)] * 3
        + [shaped(2 * BOTH, 128, dtype=F32)] + [shaped(2 * BOTH, 128)] * 3,
        [pltpu.VMEM((128, QUERIES), F32), pltpu.VMEM((QUERIES, 128), F32)], 6 * 10**9, GRADS_MIB, where,
        *taken[:2], keys_a, scores_a, products_a, keys_b, scores_b, products_b, *all_stats,
    )
    own_query, query_outs, own_keys, key_outs = outs[0], outs[1:4], outs[4], outs[5:8]
    query_terms = [near_move(query_outs[t - 1], t) for t in range(1, QUAD)]
    key_terms = [move(key_outs[t - 1], xor_j=t) for t in range(1, QUAD)]
    grad_query = (own_query + sum(t.astype(F32) for t in query_terms)).astype(BF16)
    grad_query = heads_of_own_rows(grad_query.reshape(2, ROWS, 128), core)
    regrouped = lax.all_to_all(grad_query.reshape(8, 24, 256), "head", 0, 0)
    regrouped = jnp.swapaxes(regrouped, 0, 1).reshape(24, 2048)
    both = (own_keys + sum(t.astype(F32) for t in key_terms)).astype(BF16)
    both = both.reshape(2, 2, ROWS, 128)
    grad_keys, grad_values = heads_of_own_rows(jnp.swapaxes(both, 0, 1), core)
    return regrouped, grad_keys, grad_values


def solution(mesh):
    placed = (P("seq", "head"), P("seq", "head"), P("seq", "head"), P("seq", "head"), P("seq"))
    return jax.shard_map(
        body,
        mesh=mesh,
        in_specs=placed,
        out_specs=(P(("seq", "head"), None), P("seq", "head"), P("seq", "head")),
        check_vma=False,
    )
```

profile of v0, /device:TPU:32, one launch (start us, length us, event | category | flops | bytes accessed | tf_op | source)
XLA Modules:
  0.0 102.8 jit_solution(8531662325556785159)
XLA Ops:
  0.6 0.7 fusion.7
  1.4 1.1 %pad_maximum_fusion = (bf16[400,256]{1,0:T(8,128)(2,1)S(1)}, bf16[400,256]{1,0:T(8,128)(2,1)S(1)}) fusion(bf16[16,256]{1,0:T(8,128)(2,1)S(1)} %broadcast_bitcast_fusion, bf16[192,256]{1,0:T(8,128)(2,1)} %param.7, bf16[192,256]{1,0:T(8,128)(2,1)} %param.6, bf16[192,256]{1,0:T(8,128)(2,1)} %param.8, bf16[192,256]{1,0:T(8,128)(2,1)} %param.5), kind=kLoop, calls=%fused_computation.1 | loop fusion | flops 1126400 | bytes 811008 | tf_op jit(solution)/shard_map/concatenate | solution.py:56
  2.4 1.9 %collective-permute-start.1 = (bf16[400,256]{1,0:T(8,128)(2,1)S(1)}, bf16[400,256]{1,0:T(8,128)(2,1)S(1)}, u32[]{:S(2)}, u32[]{:S(2)}) collective-permute-start(bf16[400,256]{1,0:T(8,128)(2,1)S(1)} %get-tuple-element.48.refs_0_), channel_id=1, source_target_pairs={{0,16},{8,24},{16,0},{24,8},{32,48},{40,56},{48,32},{56,40},{64,80... | collective-permute-start | bytes 614408 | tf_op jit(solution)/shard_map/ppermute | solution.py:43
  4.3 1.6 %collective-permute-start.8 = (bf16[400,256]{1,0:T(8,128)(2,1)S(1)}, bf16[400,256]{1,0:T(8,128)(2,1)S(1)}, u32[]{:S(2)}, u32[]{:S(2)}) collective-permute-start(bf16[400,256]{1,0:T(8,128)(2,1)S(1)} %get-tuple-element.47.refs_8_), channel_id=1, source_target_pairs={{0,32},{8,40},{16,48},{24,56},{32,0},{40,8},{48,16},{56,24},{64,96... | collective-permute-start | bytes 614408 | tf_op jit(solution)/shard_map/ppermute | solution.py:43
  5.9 1.5 %collective-permute-start.3 = (bf16[400,256]{1,0:T(8,128)(2,1)S(1)}, bf16[400,256]{1,0:T(8,128)(2,1)S(1)}, u32[]{:S(2)}, u32[]{:S(2)}) collective-permute-start(bf16[400,256]{1,0:T(8,128)(2,1)S(1)} %get-tuple-element.48.refs_0_), channel_id=1, source_target_pairs={{0,128},{8,136},{16,144},{24,152},{32,160},{40,168},{48,176},{56,1... | collective-permute-start | bytes 614408 | tf_op jit(solution)/shard_map/ppermute | solution.py:43
  7.4 0.0 collective-permute-start.7
  7.4 0.5 collective-permute-start
  7.9 3.9 %collective-permute-done.1.refs_2_ = bf16[400,256]{1,0:T(8,128)(2,1)S(1)} collective-permute-done((bf16[400,256]{1,0:T(8,128)(2,1)S(1)}, bf16[400,256]{1,0:T(8,128)(2,1)S(1)}, u32[]{:S(2)}, u32[]{:S(2)}) %collective-permute-start.1) | collective-permute-done | bytes 204832 | tf_op jit(solution)/shard_map/ppermute | solution.py:43
  11.8 6.9 %collective-permute-start.10 = (bf16[400,256]{1,0:T(8,128)(2,1)S(1)}, bf16[400,256]{1,0:T(8,128)(2,1)S(1)}, u32[]{:S(2)}, u32[]{:S(2)}) collective-permute-start(bf16[400,256]{1,0:T(8,128)(2,1)S(1)} %get-tuple-element.47.refs_8_), channel_id=1, source_target_pairs={{0,64},{8,72},{16,80},{24,88},{32,96},{40,104},{48,112},{56,120},{... | collective-permute-start | bytes 614408 | tf_op jit(solution)/shard_map/ppermute | solution.py:43
  18.6 0.0 collective-permute-done.8.refs_10_
  18.6 1.5 %collective-permute-start.5 = (bf16[400,256]{1,0:T(8,128)(2,1)S(1)}, bf16[400,256]{1,0:T(8,128)(2,1)S(1)}, u32[]{:S(2)}, u32[]{:S(2)}) collective-permute-start(bf16[400,256]{1,0:T(8,128)(2,1)S(1)} %collective-permute-done.1.refs_2_), channel_id=1, source_target_pairs={{0,128},{8,136},{16,144},{24,152},{32,160},{40,168},{48,176},{56,1... | collective-permute-start | bytes 614408 | tf_op jit(solution)/shard_map/ppermute | solution.py:43
  20.1 8.9 %collective-permute-start.12 = (bf16[400,256]{1,0:T(8,128)(2,1)S(1)}, bf16[400,256]{1,0:T(8,128)(2,1)S(1)}, u32[]{:S(2)}, u32[]{:S(2)}) collective-permute-start(bf16[400,256]{1,0:T(8,128)(2,1)S(1)} %get-tuple-element.47.refs_8_), channel_id=1, source_target_pairs={{0,96},{8,104},{16,112},{24,120},{32,64},{40,72},{48,80},{56,88},{... | collective-permute-start | bytes 614408 | tf_op jit(solution)/shard_map/ppermute | solution.py:43
  29.0 0.5 collective-permute-start.9
  29.5 0.1 collective-permute-start.4
  29.6 0.0 collective-permute-done.5.refs_6_
  29.6 0.4 collective-permute-start.6
  30.1 5.7 %collective-permute-done.12.refs_6_ = bf16[400,256]{1,0:T(8,128)(2,1)S(1)} collective-permute-done((bf16[400,256]{1,0:T(8,128)(2,1)S(1)}, bf16[400,256]{1,0:T(8,128)(2,1)S(1)}, u32[]{:S(2)}, u32[]{:S(2)}) %collective-permute-start.12) | collective-permute-done | bytes 204832 | tf_op jit(solution)/shard_map/ppermute | solution.py:43
  35.7 0.5 collective-permute-start.13
  36.3 0.1 pad_add_fusion.where_ref
  36.3 0.0 collective-permute-done.6.refs_7_
  36.3 3.0 %shard_map.76 = (bf16[1536,128]{1,0:T(8,128)(2,1)S(1)}, bf16[1536,128]{1,0:T(8,128)(2,1)S(1)}, f32[8,1536]{1,0:T(8,128)S(1)}, bf16[768,128]{1,0:T(8,128)(2,1)S(1...) custom-call(s32[2]{0:T(128)S(1)} %pad_add_fusion.where_ref, ...), custom_call_target="tpu_custom_call" | custom-call | flops 2000000000 | bytes 4000000 | tf_op jit(solution)/shard_map/pallas_call | solution.py:221
  39.4 0.0 collective-permute-done.11.refs_5_
  39.4 2.9 %shard_map.77 = (bf16[768,128]{1,0:T(8,128)(2,1)S(1)}, f32[768,1536]{1,0:T(8,128)S(1)}, f32[768,1536]{1,0:T(8,128)S(1)}, f32[8,1536]{1,0:T(8,128)S(1)}) custom-call(s32[2]{0:T(128)S(1)} %pad_add_fusion.where_ref, bf16[1536,128]{1,0:T(8,128)(2,1)S(1)} %get-tuple-element.22.refs_0_, bf16[1536,128]{1,0:T(8,128)(2,1)S(1)} %get-tuple-element.23.refs_1_, ...), custom_call_target="tpu_custom_call" | custom-call | flops 2000000000 | bytes 4000000 | tf_op jit(solution)/shard_map/pallas_call | solution.py:221
  42.3 0.2 collective-permute-start.14
  42.5 1.5 %collective-permute-start.15 = (f32[8,1536]{1,0:T(8,128)S(1)}, f32[8,1536]{1,0:T(8,128)S(1)}, u32[]{:S(2)}, u32[]{:S(2)}) collective-permute-start(f32[8,1536]{1,0:T(8,128)S(1)} %get-tuple-element.32.refs_8_), channel_id=1, source_target_pairs={{0,128},{8,136},{16,144},{24,152},{32,160},{40,168},{48,176},{56,1... | collective-permute-start | bytes 147464 | tf_op jit(solution)/shard_map/ppermute | solution.py:43
  44.0 1.9 %collective-permute-start.16 = (f32[8,1536]{1,0:T(8,128)S(1)}, f32[8,1536]{1,0:T(8,128)S(1)}, u32[]{:S(2)}, u32[]{:S(2)}) collective-permute-start(f32[8,1536]{1,0:T(8,128)S(1)} %get-tuple-element.32.refs_8_), channel_id=1, source_target_pairs={{0,144},{8,152},{16,128},{24,136},{32,176},{40,184},{48,160},{56,1... | collective-permute-start | bytes 147464 | tf_op jit(solution)/shard_map/ppermute | solution.py:43
  45.9 0.8 collective-permute-done.14.refs_9_
  46.7 2.3 %collective-permute-done.16.refs_11_ = f32[8,1536]{1,0:T(8,128)S(1)} collective-permute-done((f32[8,1536]{1,0:T(8,128)S(1)}, f32[8,1536]{1,0:T(8,128)S(1)}, u32[]{:S(2)}, u32[]{:S(2)}) %collective-permute-start.16) | collective-permute-done | bytes 49184 | tf_op jit(solution)/shard_map/ppermute | solution.py:43
  49.0 4.6 %shard_map.78 = (f32[384,128]{1,0:T(8,128)S(1)}, bf16[384,128]{1,0:T(8,128)(2,1)S(1)}, bf16[384,128]{1,0:T(8,128)(2,1)S(1)}, bf16[384,128]{1,0:T(8,128)(2,1)S(1)...) custom-call(s32[2]{0:T(128)S(1)} %pad_add_fusion.where_ref, ...), custom_call_target="tpu_custom_call" | custom-call | flops 6000000000 | bytes 4000000 | tf_op jit(solution)/shard_map/pallas_call | solution.py:221
  53.6 1.7 %collective-permute-start.17 = (bf16[384,128]{1,0:T(8,128)(2,1)S(1)}, bf16[384,128]{1,0:T(8,128)(2,1)S(1)}, u32[]{:S(2)}, u32[]{:S(2)}) collective-permute-start(bf16[384,128]{1,0:T(8,128)(2,1)S(1)} %get-tuple-element.34), channel_id=1, source_target_pairs={{0,16},{8,24},{16,0},{24,8},{32,48},{40,56},{48,32},{56,40},{64,80... | collective-permute-start | bytes 294920 | tf_op jit(solution)/shard_map/ppermute | solution.py:43
  55.4 0.8 collective-permute-start.18
  56.1 1.1 %collective-permute-start.19 = (bf16[384,128]{1,0:T(8,128)(2,1)S(1)}, bf16[384,128]{1,0:T(8,128)(2,1)S(1)}, u32[]{:S(2)}, u32[]{:S(2)}) collective-permute-start(bf16[384,128]{1,0:T(8,128)(2,1)S(1)} %get-tuple-element.36), channel_id=1, source_target_pairs={{0,144},{8,152},{16,128},{24,136},{32,176},{40,184},{48,160},{56,1... | collective-permute-start | bytes 294920 | tf_op jit(solution)/shard_map/ppermute | solution.py:43
  57.2 2.1 %collective-permute-done.17 = bf16[384,128]{1,0:T(8,128)(2,1)S(1)} collective-permute-done((bf16[384,128]{1,0:T(8,128)(2,1)S(1)}, bf16[384,128]{1,0:T(8,128)(2,1)S(1)}, u32[]{:S(2)}, u32[]{:S(2)}) %collective-permute-start.17) | collective-permute-done | bytes 98336 | tf_op jit(solution)/shard_map/ppermute | solution.py:43
  59.3 1.0 %collective-permute-done.18 = bf16[384,128]{1,0:T(8,128)(2,1)S(1)} collective-permute-done((bf16[384,128]{1,0:T(8,128)(2,1)S(1)}, bf16[384,128]{1,0:T(8,128)(2,1)S(1)}, u32[]{:S(2)}, u32[]{:S(2)}) %collective-permute-start.18) | collective-permute-done | bytes 98336 | tf_op jit(solution)/shard_map/ppermute | solution.py:43
  60.3 1.3 %collective-permute-done.19 = bf16[384,128]{1,0:T(8,128)(2,1)S(1)} collective-permute-done((bf16[384,128]{1,0:T(8,128)(2,1)S(1)}, bf16[384,128]{1,0:T(8,128)(2,1)S(1)}, u32[]{:S(2)}, u32[]{:S(2)}) %collective-permute-start.19) | collective-permute-done | bytes 98336 | tf_op jit(solution)/shard_map/ppermute | solution.py:43
  61.7 0.1 collective-permute-start.20
  61.8 0.7 collective-permute-start.21
  62.5 4.6 %collective-permute-start.22 = (bf16[768,128]{1,0:T(8,128)(2,1)S(1)}, bf16[768,128]{1,0:T(8,128)(2,1)S(1)}, u32[]{:S(2)}, u32[]{:S(2)}) collective-permute-start(bf16[768,128]{1,0:T(8,128)(2,1)S(1)} %get-tuple-element.39), channel_id=1, source_target_pairs={{0,64},{8,72},{16,80},{24,88},{32,96},{40,104},{48,112},{56,120},{... | collective-permute-start | bytes 589832 | tf_op jit(solution)/shard_map/ppermute | solution.py:43
  67.1 1.3 %collective-permute-start.23 = (bf16[768,128]{1,0:T(8,128)(2,1)S(1)}, bf16[768,128]{1,0:T(8,128)(2,1)S(1)}, u32[]{:S(2)}, u32[]{:S(2)}) collective-permute-start(bf16[768,128]{1,0:T(8,128)(2,1)S(1)} %get-tuple-element.40), channel_id=1, source_target_pairs={{0,96},{8,104},{16,112},{24,120},{32,64},{40,72},{48,80},{56,88},{... | collective-permute-start | bytes 589832 | tf_op jit(solution)/shard_map/ppermute | solution.py:43
  68.4 0.0 collective-permute-done.20
  68.4 11.5 %collective-permute-done.21 = bf16[768,128]{1,0:T(8,128)(2,1)S(1)} collective-permute-done((bf16[768,128]{1,0:T(8,128)(2,1)S(1)}, bf16[768,128]{1,0:T(8,128)(2,1)S(1)}, u32[]{:S(2)}, u32[]{:S(2)}) %collective-permute-start.21) | collective-permute-done | bytes 196640 | tf_op jit(solution)/shard_map/ppermute | solution.py:43
  79.9 0.0 collective-permute-done.22
  79.9 6.5 %collective-permute-done.23 = bf16[768,128]{1,0:T(8,128)(2,1)S(1)} collective-permute-done((bf16[768,128]{1,0:T(8,128)(2,1)S(1)}, bf16[768,128]{1,0:T(8,128)(2,1)S(1)}, u32[]{:S(2)}, u32[]{:S(2)}) %collective-permute-start.23) | collective-permute-done | bytes 196640 | tf_op jit(solution)/shard_map/ppermute | solution.py:43
  86.4 0.1 add_convert_fusion
  86.5 0.1 collective-permute-start.24
  86.6 14.8 %all_to_all.5 = bf16[8,24,256]{2,1,0:T(8,128)(2,1)S(1)} all-to-all(bf16[8,24,256]{2,1,0:T(8,128)(2,1)S(1)} %bitcast.28), channel_id=1, replica_groups=mesh['seq'=32,'head'=8] {'head'}, dimensions={0} | all-to-all | bytes 196608 | tf_op jit(solution)/shard_map/all_to_all | solution.py:279
  101.4 0.6 copy.9
  102.1 0.7 fusion.2
  (22 shorter events, 0.2 us)
Async XLA Ops:
  2.4 9.3 %collective-permute-start.1 = (bf16[400,256]{1,0:T(8,128)(2,1)S(1)}, bf16[400,256]{1,0:T(8,128)(2,1)S(1)}, u32[]{:S(2)}, u32[]{:S(2)}) collective-permute-start(bf16[400,256]{1,0:T(8,128)(2,1)S(1)} %get-tuple-element.48.refs_0_), channel_id=1, source_target_pairs={{0,16},{8,24},{16,0},{24,8},{32,48},{40,56},{48,32},{56,40},{64,80... | collective-permute-start | bytes 614408 | tf_op jit(solution)/shard_map/ppermute | solution.py:43
  4.3 14.3 %collective-permute-start.8 = (bf16[400,256]{1,0:T(8,128)(2,1)S(1)}, bf16[400,256]{1,0:T(8,128)(2,1)S(1)}, u32[]{:S(2)}, u32[]{:S(2)}) collective-permute-start(bf16[400,256]{1,0:T(8,128)(2,1)S(1)} %get-tuple-element.47.refs_8_), channel_id=1, source_target_pairs={{0,32},{8,40},{16,48},{24,56},{32,0},{40,8},{48,16},{56,24},{64,96... | collective-permute-start | bytes 614408 | tf_op jit(solution)/shard_map/ppermute | solution.py:43
  5.9 14.2 %collective-permute-start.3 = (bf16[400,256]{1,0:T(8,128)(2,1)S(1)}, bf16[400,256]{1,0:T(8,128)(2,1)S(1)}, u32[]{:S(2)}, u32[]{:S(2)}) collective-permute-start(bf16[400,256]{1,0:T(8,128)(2,1)S(1)} %get-tuple-element.48.refs_0_), channel_id=1, source_target_pairs={{0,128},{8,136},{16,144},{24,152},{32,160},{40,168},{48,176},{56,1... | collective-permute-start | bytes 614408 | tf_op jit(solution)/shard_map/ppermute | solution.py:43
  7.4 21.6 %collective-permute-start.7 = (bf16[400,256]{1,0:T(8,128)(2,1)S(1)}, bf16[400,256]{1,0:T(8,128)(2,1)S(1)}, u32[]{:S(2)}, u32[]{:S(2)}) collective-permute-start(bf16[400,256]{1,0:T(8,128)(2,1)S(1)} %get-tuple-element.47.refs_8_), channel_id=1, source_target_pairs={{0,8},{8,0},{16,24},{24,16},{32,40},{40,32},{48,56},{56,48},{64,72... | collective-permute-start | bytes 614408 | tf_op jit(solution)/shard_map/ppermute | solution.py:43
  7.4 21.6 %collective-permute-start = (bf16[400,256]{1,0:T(8,128)(2,1)S(1)}, bf16[400,256]{1,0:T(8,128)(2,1)S(1)}, u32[]{:S(2)}, u32[]{:S(2)}) collective-permute-start(bf16[400,256]{1,0:T(8,128)(2,1)S(1)} %get-tuple-element.48.refs_0_), channel_id=1, source_target_pairs={{0,8},{8,0},{16,24},{24,16},{32,40},{40,32},{48,56},{56,48},{64,72... | collective-permute-start | bytes 614408 | tf_op jit(solution)/shard_map/ppermute | solution.py:43
  11.8 17.8 %collective-permute-start.10 = (bf16[400,256]{1,0:T(8,128)(2,1)S(1)}, bf16[400,256]{1,0:T(8,128)(2,1)S(1)}, u32[]{:S(2)}, u32[]{:S(2)}) collective-permute-start(bf16[400,256]{1,0:T(8,128)(2,1)S(1)} %get-tuple-element.47.refs_8_), channel_id=1, source_target_pairs={{0,64},{8,72},{16,80},{24,88},{32,96},{40,104},{48,112},{56,120},{... | collective-permute-start | bytes 614408 | tf_op jit(solution)/shard_map/ppermute | solution.py:43
  18.6 11.0 %collective-permute-start.5 = (bf16[400,256]{1,0:T(8,128)(2,1)S(1)}, bf16[400,256]{1,0:T(8,128)(2,1)S(1)}, u32[]{:S(2)}, u32[]{:S(2)}) collective-permute-start(bf16[400,256]{1,0:T(8,128)(2,1)S(1)} %collective-permute-done.1.refs_2_), channel_id=1, source_target_pairs={{0,128},{8,136},{16,144},{24,152},{32,160},{40,168},{48,176},{56,1... | collective-permute-start | bytes 614408 | tf_op jit(solution)/shard_map/ppermute | solution.py:43
  20.1 15.6 %collective-permute-start.12 = (bf16[400,256]{1,0:T(8,128)(2,1)S(1)}, bf16[400,256]{1,0:T(8,128)(2,1)S(1)}, u32[]{:S(2)}, u32[]{:S(2)}) collective-permute-start(bf16[400,256]{1,0:T(8,128)(2,1)S(1)} %get-tuple-element.47.refs_8_), channel_id=1, source_target_pairs={{0,96},{8,104},{16,112},{24,120},{32,64},{40,72},{48,80},{56,88},{... | collective-permute-start | bytes 614408 | tf_op jit(solution)/shard_map/ppermute | solution.py:43
  29.0 6.7 %collective-permute-start.2 = (bf16[400,256]{1,0:T(8,128)(2,1)S(1)}, bf16[400,256]{1,0:T(8,128)(2,1)S(1)}, u32[]{:S(2)}, u32[]{:S(2)}) collective-permute-start(bf16[400,256]{1,0:T(8,128)(2,1)S(1)} %collective-permute-done.1.refs_2_), channel_id=1, source_target_pairs={{0,8},{8,0},{16,24},{24,16},{32,40},{40,32},{48,56},{56,48},{64,72... | collective-permute-start | bytes 614408 | tf_op jit(solution)/shard_map/ppermute | solution.py:43
  29.0 7.3 %collective-permute-start.9 = (bf16[400,256]{1,0:T(8,128)(2,1)S(1)}, bf16[400,256]{1,0:T(8,128)(2,1)S(1)}, u32[]{:S(2)}, u32[]{:S(2)}) collective-permute-start(bf16[400,256]{1,0:T(8,128)(2,1)S(1)} %collective-permute-done.8.refs_10_), channel_id=1, source_target_pairs={{0,8},{8,0},{16,24},{24,16},{32,40},{40,32},{48,56},{56,48},{64,72... | collective-permute-start | bytes 614408 | tf_op jit(solution)/shard_map/ppermute | solution.py:43
  29.5 6.8 %collective-permute-start.4 = (bf16[400,256]{1,0:T(8,128)(2,1)S(1)}, bf16[400,256]{1,0:T(8,128)(2,1)S(1)}, u32[]{:S(2)}, u32[]{:S(2)}) collective-permute-start(bf16[400,256]{1,0:T(8,128)(2,1)S(1)} %collective-permute-done.3.refs_4_), channel_id=1, source_target_pairs={{0,8},{8,0},{16,24},{24,16},{32,40},{40,32},{48,56},{56,48},{64,72... | collective-permute-start | bytes 614408 | tf_op jit(solution)/shard_map/ppermute | solution.py:43
  29.6 6.7 %collective-permute-start.6 = (bf16[400,256]{1,0:T(8,128)(2,1)S(1)}, bf16[400,256]{1,0:T(8,128)(2,1)S(1)}, u32[]{:S(2)}, u32[]{:S(2)}) collective-permute-start(bf16[400,256]{1,0:T(8,128)(2,1)S(1)} %collective-permute-done.5.refs_6_), channel_id=1, source_target_pairs={{0,8},{8,0},{16,24},{24,16},{32,40},{40,32},{48,56},{56,48},{64,72... | collective-permute-start | bytes 614408 | tf_op jit(solution)/shard_map/ppermute | solution.py:43
  35.7 3.6 %collective-permute-start.11 = (bf16[400,256]{1,0:T(8,128)(2,1)S(1)}, bf16[400,256]{1,0:T(8,128)(2,1)S(1)}, u32[]{:S(2)}, u32[]{:S(2)}) collective-permute-start(bf16[400,256]{1,0:T(8,128)(2,1)S(1)} %collective-permute-done.10.refs_4_), channel_id=1, source_target_pairs={{0,8},{8,0},{16,24},{24,16},{32,40},{40,32},{48,56},{56,48},{64,72... | collective-permute-start | bytes 614408 | tf_op jit(solution)/shard_map/ppermute | solution.py:43
  35.7 3.6 %collective-permute-start.13 = (bf16[400,256]{1,0:T(8,128)(2,1)S(1)}, bf16[400,256]{1,0:T(8,128)(2,1)S(1)}, u32[]{:S(2)}, u32[]{:S(2)}) collective-permute-start(bf16[400,256]{1,0:T(8,128)(2,1)S(1)} %collective-permute-done.12.refs_6_), channel_id=1, source_target_pairs={{0,8},{8,0},{16,24},{24,16},{32,40},{40,32},{48,56},{56,48},{64,72... | collective-permute-start | bytes 614408 | tf_op jit(solution)/shard_map/ppermute | solution.py:43
  42.3 4.4 %collective-permute-start.14 = (f32[8,1536]{1,0:T(8,128)S(1)}, f32[8,1536]{1,0:T(8,128)S(1)}, u32[]{:S(2)}, u32[]{:S(2)}) collective-permute-start(f32[8,1536]{1,0:T(8,128)S(1)} %get-tuple-element.32.refs_8_), channel_id=1, source_target_pairs={{0,16},{8,24},{16,0},{24,8},{32,48},{40,56},{48,32},{56,40},{64,80... | collective-permute-start | bytes 147464 | tf_op jit(solution)/shard_map/ppermute | solution.py:43
  42.5 4.2 %collective-permute-start.15 = (f32[8,1536]{1,0:T(8,128)S(1)}, f32[8,1536]{1,0:T(8,128)S(1)}, u32[]{:S(2)}, u32[]{:S(2)}) collective-permute-start(f32[8,1536]{1,0:T(8,128)S(1)} %get-tuple-element.32.refs_8_), channel_id=1, source_target_pairs={{0,128},{8,136},{16,144},{24,152},{32,160},{40,168},{48,176},{56,1... | collective-permute-start | bytes 147464 | tf_op jit(solution)/shard_map/ppermute | solution.py:43
  44.0 5.0 %collective-permute-start.16 = (f32[8,1536]{1,0:T(8,128)S(1)}, f32[8,1536]{1,0:T(8,128)S(1)}, u32[]{:S(2)}, u32[]{:S(2)}) collective-permute-start(f32[8,1536]{1,0:T(8,128)S(1)} %get-tuple-element.32.refs_8_), channel_id=1, source_target_pairs={{0,144},{8,152},{16,128},{24,136},{32,176},{40,184},{48,160},{56,1... | collective-permute-start | bytes 147464 | tf_op jit(solution)/shard_map/ppermute | solution.py:43
  53.6 5.6 %collective-permute-start.17 = (bf16[384,128]{1,0:T(8,128)(2,1)S(1)}, bf16[384,128]{1,0:T(8,128)(2,1)S(1)}, u32[]{:S(2)}, u32[]{:S(2)}) collective-permute-start(bf16[384,128]{1,0:T(8,128)(2,1)S(1)} %get-tuple-element.34), channel_id=1, source_target_pairs={{0,16},{8,24},{16,0},{24,8},{32,48},{40,56},{48,32},{56,40},{64,80... | collective-permute-start | bytes 294920 | tf_op jit(solution)/shard_map/ppermute | solution.py:43
  55.4 4.9 %collective-permute-start.18 = (bf16[384,128]{1,0:T(8,128)(2,1)S(1)}, bf16[384,128]{1,0:T(8,128)(2,1)S(1)}, u32[]{:S(2)}, u32[]{:S(2)}) collective-permute-start(bf16[384,128]{1,0:T(8,128)(2,1)S(1)} %get-tuple-element.35), channel_id=1, source_target_pairs={{0,128},{8,136},{16,144},{24,152},{32,160},{40,168},{48,176},{56,1... | collective-permute-start | bytes 294920 | tf_op jit(solution)/shard_map/ppermute | solution.py:43
  56.1 5.5 %collective-permute-start.19 = (bf16[384,128]{1,0:T(8,128)(2,1)S(1)}, bf16[384,128]{1,0:T(8,128)(2,1)S(1)}, u32[]{:S(2)}, u32[]{:S(2)}) collective-permute-start(bf16[384,128]{1,0:T(8,128)(2,1)S(1)} %get-tuple-element.36), channel_id=1, source_target_pairs={{0,144},{8,152},{16,128},{24,136},{32,176},{40,184},{48,160},{56,1... | collective-permute-start | bytes 294920 | tf_op jit(solution)/shard_map/ppermute | solution.py:43
  61.7 6.7 %collective-permute-start.20 = (bf16[192,128]{1,0:T(8,128)(2,1)S(1)}, bf16[192,128]{1,0:T(8,128)(2,1)S(1)}, u32[]{:S(2)}, u32[]{:S(2)}) collective-permute-start(bf16[192,128]{1,0:T(8,128)(2,1)S(1)} %dynamic-slice_bitcast_fusion.1), channel_id=1, source_target_pairs={{0,8},{8,0},{16,24},{24,16},{32,40},{40,32},{48,56},{56,48},{64,72... | collective-permute-start | bytes 147464 | tf_op jit(solution)/shard_map/ppermute | solution.py:43
  61.8 18.1 %collective-permute-start.21 = (bf16[768,128]{1,0:T(8,128)(2,1)S(1)}, bf16[768,128]{1,0:T(8,128)(2,1)S(1)}, u32[]{:S(2)}, u32[]{:S(2)}) collective-permute-start(bf16[768,128]{1,0:T(8,128)(2,1)S(1)} %get-tuple-element.38), channel_id=1, source_target_pairs={{0,32},{8,40},{16,48},{24,56},{32,0},{40,8},{48,16},{56,24},{64,96... | collective-permute-start | bytes 589832 | tf_op jit(solution)/shard_map/ppermute | solution.py:43
  62.5 17.4 %collective-permute-start.22 = (bf16[768,128]{1,0:T(8,128)(2,1)S(1)}, bf16[768,128]{1,0:T(8,128)(2,1)S(1)}, u32[]{:S(2)}, u32[]{:S(2)}) collective-permute-start(bf16[768,128]{1,0:T(8,128)(2,1)S(1)} %get-tuple-element.39), channel_id=1, source_target_pairs={{0,64},{8,72},{16,80},{24,88},{32,96},{40,104},{48,112},{56,120},{... | collective-permute-start | bytes 589832 | tf_op jit(solution)/shard_map/ppermute | solution.py:43
  67.1 19.3 %collective-permute-start.23 = (bf16[768,128]{1,0:T(8,128)(2,1)S(1)}, bf16[768,128]{1,0:T(8,128)(2,1)S(1)}, u32[]{:S(2)}, u32[]{:S(2)}) collective-permute-start(bf16[768,128]{1,0:T(8,128)(2,1)S(1)} %get-tuple-element.40), channel_id=1, source_target_pairs={{0,96},{8,104},{16,112},{24,120},{32,64},{40,72},{48,80},{56,88},{... | collective-permute-start | bytes 589832 | tf_op jit(solution)/shard_map/ppermute | solution.py:43
  86.5 15.5 %collective-permute-start.24 = (bf16[2,192,128]{2,1,0:T(8,128)(2,1)S(1)}, bf16[2,192,128]{2,1,0:T(8,128)(2,1)S(1)}, u32[]{:S(2)}, u32[]{:S(2)}) collective-permute-start(bf16[2,192,128]{2,1,0:T(8,128)(2,1)S(1)} %dynamic-slice_bitcast_fusion), channel_id=1, source_target_pairs={{0,8},{8,0},{16,24},{24,16},{32,40},{40,32},{48,56},{56,48},{64,72... | collective-permute-start | bytes 294920 | tf_op jit(solution)/shard_map/ppermute | solution.py:43
where the time goes:
time: 103 us
  starting transfers between devices  38.2 us (37%)
  waiting for transfers between devices  35.1 us (34%)
  blocking collectives  14.8 us (14%)
  Pallas kernels  10.5 us (10%)
  other arithmetic  2.73 us (3%)
    ppermute x25, starting transfers between devices, move(): return lax.ppermute(value, 'seq', perm(**how))  38.2 us
    ppermute x25, waiting for transfers between devices, move(): return lax.ppermute(value, 'seq', perm(**how))  35.1 us
    all_to_all x1, blocking collectives, body(): regrouped = lax.all_to_all(grad_query.reshape(8, 24, 256), 'head', 0, 0)  14.8 us
    pallas_call x3, Pallas kernels, call(): pl.pallas_call(kernel, out_shape=tuple(outs), in_specs=[pl.BlockSpec(memo...  10.5 us
  transfers between devices with their start and end apart: 25, of which 9 were waited for; matrix products, arithmetic and copies ran while one was open for 1% of the time, Pallas kernels for 3%

commit v1 on v0

--- a/solution.py
+++ b/solution.py
@@ -9,11 +9,11 @@
 
 HEAD_DIM = 128
 ROWS = 192
+TAGS = 16
 BOTH = 2 * ROWS
 QUAD = 4
 QUERIES = QUAD * BOTH
-HALF_KEYS = 2 * BOTH
-TILE = 256
+MID, LAST = 3, 2
 FIRST_MIB = 16
 GRADS_MIB = 16
 LOG2E = 1.4426950408889634
@@ -53,17 +53,21 @@
     tags = jnp.stack([high, low])
     tags = jnp.pad(tags, ((0, 0), (0, 2 * HEAD_DIM - ROWS)))
     tags = jnp.broadcast_to(tags[:, None, :], (2, 8, 2 * HEAD_DIM)).reshape(16, 2 * HEAD_DIM)
-    return jnp.concatenate([first, second, tags], axis=0)
+    return jnp.concatenate([tags, first, second], axis=0)
 
 
 def places(packed_ref):
-    tags = packed_ref[BOTH : BOTH + 16, :].astype(F32)
+    tags = packed_ref[0:TAGS, :].astype(F32)
     return tags[0:8] * 128.0 + tags[8:16]
 
 
 def split(packed_ref, cols, first, second, start):
-    first[pl.ds(start, ROWS), :] = packed_ref[0:ROWS, cols]
-    second[pl.ds(start, ROWS), :] = packed_ref[ROWS:BOTH, cols]
+    if isinstance(packed_ref, tuple):
+        head, tail, base = *packed_ref, 0
+    else:
+        head, tail, base = packed_ref, packed_ref, TAGS + ROWS
+    first[pl.ds(start, ROWS), :] = head[TAGS : TAGS + ROWS, cols]
+    second[pl.ds(start, ROWS), :] = tail[base : base + ROWS, cols]
 
 
 def head_cols(core):
@@ -92,35 +96,42 @@
 
 def take_keys(where_ref, refs, keys, values, key_pos):
     core = where_ref[1]
-    for n in range(4):
+    for n in range(len(refs)):
         start = pl.multiple_of((n // 2) * BOTH + (core ^ (n % 2)) * ROWS, 64)
         split(refs[n], head_cols(core), keys, values, start)
-        tall = jnp.concatenate([places(refs[n])] * 16, axis=0)
+        tagged = refs[n][0] if isinstance(refs[n], tuple) else refs[n]
+        tall = jnp.concatenate([places(tagged)] * 16, axis=0)
         key_pos[pl.ds(start, 128), :] = jnp.transpose(tall[:, 0:128])
         key_pos[pl.ds(start + 128, 64), :] = jnp.transpose(tall[:, 128:256])[0:64]
 
 
+def tile_of(keys):
+    return 256 if keys.shape[0] % 256 == 0 else 192
+
+
 def dot_t(a, b):
     return lax.dot_general(a, b, (((1,), (1,)), ((), ())), preferred_element_type=F32)
 
 
-def masked_scores(queries, keys, query_pos, key_pos, start):
-    s = dot_t(keys[pl.ds(start, TILE), :], queries[...])
-    s = s.reshape(TILE // 8, 8, QUERIES) * (SCALE * LOG2E)
-    place = key_pos[pl.ds(start, TILE), :].reshape(TILE // 8, 8, 128)
+def masked_scores(queries, keys, query_pos, key_pos, start, tile):
+    s = dot_t(keys[pl.ds(start, tile), :], queries[...])
+    s = s.reshape(tile // 8, 8, QUERIES) * (SCALE * LOG2E)
+    place = key_pos[pl.ds(start, tile), :].reshape(tile // 8, 8, 128)
     place = jnp.concatenate([place] * (QUERIES // 128), axis=2)
     return jnp.where(place <= query_pos[...][None], s, LOW)
 
 
 def sweep(queries, grads, query_pos, keys, values, key_pos, scores, products, running):
+    tile = tile_of(keys)
+
     def turn(i, running):
         top, total, delta = running
-        start = pl.multiple_of(i * TILE, TILE)
-        s = masked_scores(queries, keys, query_pos, key_pos, start)
-        g = dot_t(values[pl.ds(start, TILE), :], grads[...])
-        scores[pl.ds(start, TILE), :] = s.reshape(TILE, QUERIES)
-        products[pl.ds(start, TILE), :] = g
-        g = g.reshape(TILE // 8, 8, QUERIES)
+        start = pl.multiple_of(i * tile, tile)
+        s = masked_scores(queries, keys, query_pos, key_pos, start, tile)
+        g = dot_t(values[pl.ds(start, tile), :], grads[...])
+        scores[pl.ds(start, tile), :] = s.reshape(tile, QUERIES)
+        products[pl.ds(start, tile), :] = g
+        g = g.reshape(tile // 8, 8, QUERIES)
         new = jnp.maximum(top, jnp.max(s, axis=0))
         shrink = jnp.exp2(top - new)
         p = jnp.exp2(s - new[None])
@@ -128,7 +139,7 @@
         delta = delta * shrink + jnp.sum(p * g, axis=0)
         return new, total, delta
 
-    return lax.fori_loop(0, HALF_KEYS // TILE, turn, running)
+    return lax.fori_loop(0, keys.shape[0] // tile, turn, running)
 
 
 def first_kernel(where_ref, *refs):
@@ -146,13 +157,19 @@
         out[n] = found[n]
 
 
-def second_kernel(where_ref, *refs):
+def later_kernel(last, where_ref, *refs):
     queries, grads, query_pos, before = refs[0:4]
-    key_refs = refs[4:8]
-    keys, scores, products, out, values, key_pos = refs[8:]
+    if last:
+        key_refs, refs = ((refs[4], refs[5]), (refs[6], refs[7])), refs[8:]
+    else:
+        key_refs, refs = refs[4:6], refs[6:]
+    keys, scores, products, out, values, key_pos = refs
     take_keys(where_ref, key_refs, keys, values, key_pos)
     running = (before[0], before[1], before[2])
     top, total, delta = sweep(queries, grads, query_pos, keys, values, key_pos, scores, products, running)
+    if not last:
+        out[0], out[1], out[2] = top, total, delta
+        return
     best = jnp.max(top, axis=0, keepdims=True)
     shrink = jnp.exp2(top - best)
     out[0:1, :] = best
@@ -163,11 +180,11 @@
 
 def grads_kernel(where_ref, *refs):
     queries, grads = refs[0:2]
-    key_refs = refs[2:8]
-    stat_refs = refs[8:12]
-    own_query, query_outs = refs[12], refs[13:16]
-    own_keys, key_outs = refs[16], refs[17:20]
-    query_sum, query_rows = refs[20:]
+    key_refs = refs[2:11]
+    stat_refs = refs[11:15]
+    own_query, query_outs = refs[15], refs[16:19]
+    own_keys, key_outs = refs[19], refs[20:23]
+    query_sum, query_rows = refs[23:]
     mine = where_ref[0]
     stats = [r[...] for r in stat_refs]
     tops = [s[0:1] for s in stats]
@@ -178,25 +195,26 @@
     log_total = jnp.broadcast_to(best + jnp.log2(total), (8, QUERIES))
     delta = jnp.broadcast_to(delta, (8, QUERIES))
     query_sum[...] = jnp.zeros_like(query_sum)
-    for part in range(2):
+    for part, targets in enumerate(((own_keys, key_outs[0]), (key_outs[1],), (key_outs[2],))):
         keys, scores, products = key_refs[3 * part : 3 * part + 3]
-        for n in range(HALF_KEYS // TILE):
-            start = n * TILE
-            s = scores[start : start + TILE, :].reshape(TILE // 8, 8, QUERIES)
-            g = products[start : start + TILE, :].reshape(TILE // 8, 8, QUERIES)
+        tile = tile_of(keys)
+        for n in range(keys.shape[0] // tile):
+            start = n * tile
+            s = scores[start : start + tile, :].reshape(tile // 8, 8, QUERIES)
+            g = products[start : start + tile, :].reshape(tile // 8, 8, QUERIES)
             p = jnp.exp2(s - log_total[None])
-            d = (p * (g - delta[None])).reshape(TILE, QUERIES).astype(BF16)
-            p = p.reshape(TILE, QUERIES).astype(BF16)
+            d = (p * (g - delta[None])).reshape(tile, QUERIES).astype(BF16)
+            p = p.reshape(tile, QUERIES).astype(BF16)
             grad_value = jnp.dot(p, grads[...], preferred_element_type=F32)
             grad_key = jnp.dot(d, queries[...], preferred_element_type=F32) * SCALE
-            keys_t = jnp.transpose(keys[start : start + TILE, :])
+            keys_t = jnp.transpose(keys[start : start + tile, :])
             query_sum[...] += jnp.dot(keys_t, d, preferred_element_type=F32)
             at = 0
-            while at < TILE:
+            while at < tile:
                 row = start + at
-                chunk, inside = 2 * part + row // BOTH, row % BOTH
-                size = min(TILE - at, BOTH - inside)
-                target = own_keys if chunk == 0 else key_outs[chunk - 1]
+                chunk, inside = row // BOTH, row % BOTH
+                size = min(tile - at, BOTH - inside)
+                target = targets[chunk]
                 target[inside : inside + size, :] = grad_key[at : at + size].astype(target.dtype)
                 target[BOTH + inside : BOTH + inside + size, :] = grad_value[at : at + size].astype(target.dtype)
                 at += size
@@ -244,24 +262,36 @@
     where = jnp.stack([(place // 16) * 2 + (place // 2) % 2, core]).astype(jnp.int32)
     key_pack = pack(key_rows, value_rows, positions)
     query_pack = pack(query_rows, grad_output, positions)
-    key_packs = [key_pack] + [move(key_pack, xor_j=t) for t in range(1, 4)]
+    key_near = {t: move(key_pack, xor_j=t) for t in (1, 3)}
     query_z = move(query_pack, xor_half=1)
     query_x = move(query_pack, xor_x=1)
     query_packs = [query_pack, query_z, query_x, move(query_z, xor_x=1)]
-    all_keys = [v for k in key_packs for v in (k, move(k, xor_core=1))]
+    head = move(key_near[3][: TAGS + ROWS], xor_j=1)
+    tail = move(key_near[1][TAGS + ROWS :], xor_j=3)
+    far_keys = (head, tail, move(head, xor_core=1), move(tail, xor_core=1))
+    all_keys = [v for k in (key_pack, key_near[1], key_near[3]) for v in (k, move(k, xor_core=1))]
     all_queries = [v for q in query_packs for v in (q, move(q, xor_core=1))]
 
     rows = [shaped(QUERIES, 128), shaped(QUERIES, 128), shaped(8, QUERIES, dtype=F32)]
-    tall = shaped(HALF_KEYS, QUERIES, dtype=F32)
-    half = [shaped(HALF_KEYS, 128), tall, tall]
-    spare = [pltpu.VMEM((HALF_KEYS, 128), BF16), pltpu.VMEM((HALF_KEYS, 128), F32)]
-    *taken, keys_a, scores_a, products_a, running = call(
-        first_kernel, rows + half + [shaped(3, 8, QUERIES, dtype=F32)], spare, 2 * 10**9, FIRST_MIB, where,
+
+    def part_of(rows):
+        outs = [shaped(rows, 128), *[shaped(rows, QUERIES, dtype=F32)] * 2]
+        return outs, [pltpu.VMEM((rows, 128), BF16), pltpu.VMEM((rows, 128), F32)]
+
+    running = shaped(3, 8, QUERIES, dtype=F32)
+    outs, spare = part_of(2 * BOTH)
+    *taken, keys_a, scores_a, products_a, found = call(
+        first_kernel, rows + outs + [running], spare, 2 * 10**9, FIRST_MIB, where,
         *all_queries, *all_keys[:4],
     )
+    outs, spare = part_of(BOTH)
+    keys_c, scores_c, products_c, found = call(
+        functools.partial(later_kernel, False), outs + [running], spare, 10**9, FIRST_MIB, where,
+        *taken, found, *all_keys[4:6],
+    )
     keys_b, scores_b, products_b, stats = call(
-        second_kernel, half + [shaped(8, QUERIES, dtype=F32)], spare, 2 * 10**9, FIRST_MIB, where,
-        *taken, running, *all_keys[4:],
+        functools.partial(later_kernel, True), outs + [shaped(8, QUERIES, dtype=F32)], spare, 10**9, FIRST_MIB,
+        where, *taken, found, *far_keys,
     )
     all_stats = [stats] + [near_move(stats, t) for t in range(1, QUAD)]
     outs = call(
@@ -269,11 +299,11 @@
         [shaped(BOTH, 128, dtype=F32)] + [shaped(BOTH, 128)] * 3
         + [shaped(2 * BOTH, 128, dtype=F32)] + [shaped(2 * BOTH, 128)] * 3,
         [pltpu.VMEM((128, QUERIES), F32), pltpu.VMEM((QUERIES, 128), F32)], 6 * 10**9, GRADS_MIB, where,
-        *taken[:2], keys_a, scores_a, products_a, keys_b, scores_b, products_b, *all_stats,
+        *taken[:2], keys_a, scores_a, products_a, keys_c, scores_c, products_c, keys_b, scores_b, products_b, *all_stats,
     )
     own_query, query_outs, own_keys, key_outs = outs[0], outs[1:4], outs[4], outs[5:8]
     query_terms = [near_move(query_outs[t - 1], t) for t in range(1, QUAD)]
-    key_terms = [move(key_outs[t - 1], xor_j=t) for t in range(1, QUAD)]
+    key_terms = [move(out, xor_j=t) for out, t in zip(key_outs, (1, MID, LAST))]
     grad_query = (own_query + sum(t.astype(F32) for t in query_terms)).astype(BF16)
     grad_query = heads_of_own_rows(grad_query.reshape(2, ROWS, 128), core)
     regrouped = lax.all_to_all(grad_query.reshape(8, 24, 256), "head", 0, 0)

time: 103 us -> 98.1 us (0.952)
  starting transfers between devices: 38.2 us -> 33.3 us
    ppermute x25 -> x27, starting transfers between devices: 38.2 us -> 33.3 us  [move(): return lax.ppermute(value, 'seq', perm(**how))]
    ppermute x25 -> x27, waiting for transfers between devices: 35.1 us -> 34.2 us  [move(): return lax.ppermute(value, 'seq', perm(**how))]
    pallas_call x3 -> x4, Pallas kernels: 10.5 us -> 11.4 us  [call(): pl.pallas_call(kernel, out_shape=tuple(outs), in_specs=[pl.BlockSpec(memo...]
  transfers between devices with their start and end apart: 25 -> 27, of which waited for: 9 -> 12; matrix products, arithmetic and copies ran while one was open for 1% -> 1% of each run, Pallas kernels for 3% -> 5%
where the time goes in v1:
time: 98.1 us; the launch traced here: 97.9 us
  waiting for transfers between devices  34.2 us (35%)
  starting transfers between devices  33.3 us (34%)
  blocking collectives  14.7 us (15%)
  Pallas kernels  11.4 us (12%)
  other arithmetic  2.73 us (3%)
    ppermute x27, waiting for transfers between devices, move(): return lax.ppermute(value, 'seq', perm(**how))  34.2 us
    ppermute x27, starting transfers between devices, move(): return lax.ppermute(value, 'seq', perm(**how))  33.3 us
    all_to_all x1, blocking collectives, body(): regrouped = lax.all_to_all(grad_query.reshape(8, 24, 256), 'head', 0, 0)  14.7 us
    pallas_call x4, Pallas kernels, call(): pl.pallas_call(kernel, out_shape=tuple(outs), in_specs=[pl.BlockSpec(memo...  11.4 us
  transfers between devices with their start and end apart: 27, of which 12 were waited for; matrix products, arithmetic and copies ran while one was open for 1% of the time, Pallas kernels for 5%

profile of v1, /device:TPU:32, one launch (start us, length us, event | category | flops | bytes accessed | tf_op | source)
XLA Modules:
  0.0 97.9 jit_solution(15519761127499806331)
XLA Ops:
  0.6 0.7 fusion.9
  1.4 1.1 %fusion.1 = (bf16[400,256]{1,0:T(8,128)(2,1)S(1)}, bf16[400,256]{1,0:T(8,128)(2,1)S(1)}) fusion(bf16[16,256]{1,0:T(8,128)(2,1)S(1)} %broadcast_bitcast_fusion, bf16[192,256]{1,0:T(8,128)(2,1)} %param.7, bf16[192,256]{1,0:T(8,128)(2,1)} %param.6, bf16[192,256]{1,0:T(8,128)(2,1)} %param.8, bf16[192,256]{1,0:T(8,128)(2,1)} %param.5), kind=kLoop, calls=%fused_computation.4 | loop fusion | flops 1126400 | bytes 811008 | tf_op jit(solution)/shard_map/concatenate | solution.py:56
  2.4 1.9 %collective-permute-start.1 = (bf16[400,256]{1,0:T(8,128)(2,1)S(1)}, bf16[400,256]{1,0:T(8,128)(2,1)S(1)}, u32[]{:S(2)}, u32[]{:S(2)}) collective-permute-start(bf16[400,256]{1,0:T(8,128)(2,1)S(1)} %get-tuple-element.56.refs_0_), channel_id=1, source_target_pairs={{0,16},{8,24},{16,0},{24,8},{32,48},{40,56},{48,32},{56,40},{64,80... | collective-permute-start | bytes 614408 | tf_op jit(solution)/shard_map/ppermute | solution.py:43
  4.3 1.6 %collective-permute-start.8 = (bf16[400,256]{1,0:T(8,128)(2,1)S(1)}, bf16[400,256]{1,0:T(8,128)(2,1)S(1)}, u32[]{:S(2)}, u32[]{:S(2)}) collective-permute-start(bf16[400,256]{1,0:T(8,128)(2,1)S(1)} %get-tuple-element.55.refs_8_), channel_id=1, source_target_pairs={{0,32},{8,40},{16,48},{24,56},{32,0},{40,8},{48,16},{56,24},{64,96... | collective-permute-start | bytes 614408 | tf_op jit(solution)/shard_map/ppermute | solution.py:43
  5.9 4.5 %collective-permute-start.10 = (bf16[400,256]{1,0:T(8,128)(2,1)S(1)}, bf16[400,256]{1,0:T(8,128)(2,1)S(1)}, u32[]{:S(2)}, u32[]{:S(2)}) collective-permute-start(bf16[400,256]{1,0:T(8,128)(2,1)S(1)} %get-tuple-element.55.refs_8_), channel_id=1, source_target_pairs={{0,96},{8,104},{16,112},{24,120},{32,64},{40,72},{48,80},{56,88},{... | collective-permute-start | bytes 614408 | tf_op jit(solution)/shard_map/ppermute | solution.py:43
  10.4 1.5 %collective-permute-start.3 = (bf16[400,256]{1,0:T(8,128)(2,1)S(1)}, bf16[400,256]{1,0:T(8,128)(2,1)S(1)}, u32[]{:S(2)}, u32[]{:S(2)}) collective-permute-start(bf16[400,256]{1,0:T(8,128)(2,1)S(1)} %get-tuple-element.56.refs_0_), channel_id=1, source_target_pairs={{0,128},{8,136},{16,144},{24,152},{32,160},{40,168},{48,176},{56,1... | collective-permute-start | bytes 614408 | tf_op jit(solution)/shard_map/ppermute | solution.py:43
  11.9 0.0 collective-permute-start
  11.9 1.5 %collective-permute-done.1.refs_2_ = bf16[400,256]{1,0:T(8,128)(2,1)S(1)} collective-permute-done((bf16[400,256]{1,0:T(8,128)(2,1)S(1)}, bf16[400,256]{1,0:T(8,128)(2,1)S(1)}, u32[]{:S(2)}, u32[]{:S(2)}) %collective-permute-start.1) | collective-permute-done | bytes 204832 | tf_op jit(solution)/shard_map/ppermute | solution.py:43
  13.4 0.0 collective-permute-start.7
  13.4 6.3 %collective-permute-done.8.refs_10_ = bf16[400,256]{1,0:T(8,128)(2,1)S(1)} collective-permute-done((bf16[400,256]{1,0:T(8,128)(2,1)S(1)}, bf16[400,256]{1,0:T(8,128)(2,1)S(1)}, u32[]{:S(2)}, u32[]{:S(2)}) %collective-permute-start.8) | collective-permute-done | bytes 204832 | tf_op jit(solution)/shard_map/ppermute | solution.py:43
  19.6 1.5 %collective-permute-start.5 = (bf16[400,256]{1,0:T(8,128)(2,1)S(1)}, bf16[400,256]{1,0:T(8,128)(2,1)S(1)}, u32[]{:S(2)}, u32[]{:S(2)}) collective-permute-start(bf16[400,256]{1,0:T(8,128)(2,1)S(1)} %collective-permute-done.1.refs_2_), channel_id=1, source_target_pairs={{0,128},{8,136},{16,144},{24,152},{32,160},{40,168},{48,176},{56,1... | collective-permute-start | bytes 614408 | tf_op jit(solution)/shard_map/ppermute | solution.py:43
  21.1 0.0 collective-permute-done.10.refs_4_
  21.2 2.5 %collective-permute-start.13 = (bf16[192,256]{1,0:T(8,128)(2,1)S(1)}, bf16[192,256]{1,0:T(8,128)(2,1)S(1)}, u32[]{:S(2)}, u32[]{:S(2)}) collective-permute-start(bf16[192,256]{1,0:T(8,128)(2,1)S(1)} %slice.9), channel_id=1, source_target_pairs={{0,96},{8,104},{16,112},{24,120},{32,64},{40,72},{48,80},{56,88},{... | collective-permute-start | bytes 294920 | tf_op jit(solution)/shard_map/ppermute | solution.py:43
  23.7 3.4 %collective-permute-start.12 = (bf16[208,256]{1,0:T(8,128)(2,1)S(1)}, bf16[208,256]{1,0:T(8,128)(2,1)S(1)}, u32[]{:S(2)}, u32[]{:S(2)}) collective-permute-start(bf16[208,256]{1,0:T(8,128)(2,1)S(1)} %slice.8), channel_id=1, source_target_pairs={{0,32},{8,40},{16,48},{24,56},{32,0},{40,8},{48,16},{56,24},{64,96... | collective-permute-start | bytes 319496 | tf_op jit(solution)/shard_map/ppermute | solution.py:43
  27.1 0.5 collective-permute-start.9
  27.6 0.7 collective-permute-done.13.refs_5_
  28.4 0.5 collective-permute-start.6
  28.9 1.0 collective-permute-done.12.refs_4_
  29.8 0.1 pad_add_fusion.where_ref
  29.9 0.5 collective-permute-start.15
  30.4 0.1 collective-permute-start.14
  30.6 3.0 %shard_map.76 = (bf16[1536,128]{1,0:T(8,128)(2,1)S(1)}, bf16[1536,128]{1,0:T(8,128)(2,1)S(1)}, f32[8,1536]{1,0:T(8,128)S(1)}, bf16[768,128]{1,0:T(8,128)(2,1)S(1...) custom-call(s32[2]{0:T(128)S(1)} %pad_add_fusion.where_ref, ...), custom_call_target="tpu_custom_call" | custom-call | flops 2000000000 | bytes 4000000 | tf_op jit(solution)/shard_map/pallas_call | solution.py:239
  33.6 1.8 %shard_map.77 = (bf16[384,128]{1,0:T(8,128)(2,1)S(1)}, f32[384,1536]{1,0:T(8,128)S(1)}, f32[384,1536]{1,0:T(8,128)S(1)}, f32[3,8,1536]{2,1,0:T(8,128)S(1)}) custom-call(s32[2]{0:T(128)S(1)} %pad_add_fusion.where_ref, bf16[1536,128]{1,0:T(8,128)(2,1)S(1)} %get-tuple-element.26.refs_0_, bf16[1536,128]{1,0:T(8,128)(2,1)S(1)} %get-tuple-element.27.refs_1_, ...), custom_call_target="tpu_custom_call" | custom-call | flops 1000000000 | bytes 4000000 | tf_op jit(solution)/shard_map/pallas_call | solution.py:239
  35.4 1.9 %shard_map.78 = (bf16[384,128]{1,0:T(8,128)(2,1)S(1)}, f32[384,1536]{1,0:T(8,128)S(1)}, f32[384,1536]{1,0:T(8,128)S(1)}, f32[8,1536]{1,0:T(8,128)S(1)}) custom-call(s32[2]{0:T(128)S(1)} %pad_add_fusion.where_ref, bf16[1536,128]{1,0:T(8,128)(2,1)S(1)} %get-tuple-element.26.refs_0_, bf16[1536,128]{1,0:T(8,128)(2,1)S(1)} %get-tuple-element.27.refs_1_, ...), custom_call_target="tpu_custom_call" | custom-call | flops 1000000000 | bytes 4000000 | tf_op jit(solution)/shard_map/pallas_call | solution.py:239
  37.3 2.7 %collective-permute-start.16 = (f32[8,1536]{1,0:T(8,128)S(1)}, f32[8,1536]{1,0:T(8,128)S(1)}, u32[]{:S(2)}, u32[]{:S(2)}) collective-permute-start(f32[8,1536]{1,0:T(8,128)S(1)} %get-tuple-element.40.refs_11_), channel_id=1, source_target_pairs={{0,16},{8,24},{16,0},{24,8},{32,48},{40,56},{48,32},{56,40},{64,80... | collective-permute-start | bytes 147464 | tf_op jit(solution)/shard_map/ppermute | solution.py:43
  40.0 0.6 collective-permute-start.17
  40.6 1.1 %collective-permute-start.18 = (f32[8,1536]{1,0:T(8,128)S(1)}, f32[8,1536]{1,0:T(8,128)S(1)}, u32[]{:S(2)}, u32[]{:S(2)}) collective-permute-start(f32[8,1536]{1,0:T(8,128)S(1)} %get-tuple-element.40.refs_11_), channel_id=1, source_target_pairs={{0,144},{8,152},{16,128},{24,136},{32,176},{40,184},{48,160},{56,1... | collective-permute-start | bytes 147464 | tf_op jit(solution)/shard_map/ppermute | solution.py:43
  41.7 0.6 collective-permute-done.16.refs_12_
  42.3 2.3 %collective-permute-done.17.refs_13_ = f32[8,1536]{1,0:T(8,128)S(1)} collective-permute-done((f32[8,1536]{1,0:T(8,128)S(1)}, f32[8,1536]{1,0:T(8,128)S(1)}, u32[]{:S(2)}, u32[]{:S(2)}) %collective-permute-start.17) | collective-permute-done | bytes 49184 | tf_op jit(solution)/shard_map/ppermute | solution.py:43
  44.6 1.0 %collective-permute-done.18.refs_14_ = f32[8,1536]{1,0:T(8,128)S(1)} collective-permute-done((f32[8,1536]{1,0:T(8,128)S(1)}, f32[8,1536]{1,0:T(8,128)S(1)}, u32[]{:S(2)}, u32[]{:S(2)}) %collective-permute-start.18) | collective-permute-done | bytes 49184 | tf_op jit(solution)/shard_map/ppermute | solution.py:43
  45.6 4.7 %shard_map.79 = (f32[384,128]{1,0:T(8,128)S(1)}, bf16[384,128]{1,0:T(8,128)(2,1)S(1)}, bf16[384,128]{1,0:T(8,128)(2,1)S(1)}, bf16[384,128]{1,0:T(8,128)(2,1)S(1)...) custom-call(s32[2]{0:T(128)S(1)} %pad_add_fusion.where_ref, ...), custom_call_target="tpu_custom_call" | custom-call | flops 6000000000 | bytes 4000000 | tf_op jit(solution)/shard_map/pallas_call | solution.py:239
  50.3 0.4 collective-permute-start.19
  50.6 1.4 %collective-permute-start.20 = (bf16[384,128]{1,0:T(8,128)(2,1)S(1)}, bf16[384,128]{1,0:T(8,128)(2,1)S(1)}, u32[]{:S(2)}, u32[]{:S(2)}) collective-permute-start(bf16[384,128]{1,0:T(8,128)(2,1)S(1)} %get-tuple-element.43), channel_id=1, source_target_pairs={{0,128},{8,136},{16,144},{24,152},{32,160},{40,168},{48,176},{56,1... | collective-permute-start | bytes 294920 | tf_op jit(solution)/shard_map/ppermute | solution.py:43
  52.0 1.8 %collective-permute-start.21 = (bf16[384,128]{1,0:T(8,128)(2,1)S(1)}, bf16[384,128]{1,0:T(8,128)(2,1)S(1)}, u32[]{:S(2)}, u32[]{:S(2)}) collective-permute-start(bf16[384,128]{1,0:T(8,128)(2,1)S(1)} %get-tuple-element.44), channel_id=1, source_target_pairs={{0,144},{8,152},{16,128},{24,136},{32,176},{40,184},{48,160},{56,1... | collective-permute-start | bytes 294920 | tf_op jit(solution)/shard_map/ppermute | solution.py:43
  53.8 1.3 %collective-permute-done.19 = bf16[384,128]{1,0:T(8,128)(2,1)S(1)} collective-permute-done((bf16[384,128]{1,0:T(8,128)(2,1)S(1)}, bf16[384,128]{1,0:T(8,128)(2,1)S(1)}, u32[]{:S(2)}, u32[]{:S(2)}) %collective-permute-start.19) | collective-permute-done | bytes 98336 | tf_op jit(solution)/shard_map/ppermute | solution.py:43
  55.1 0.9 collective-permute-done.20
  56.0 1.5 %collective-permute-done.21 = bf16[384,128]{1,0:T(8,128)(2,1)S(1)} collective-permute-done((bf16[384,128]{1,0:T(8,128)(2,1)S(1)}, bf16[384,128]{1,0:T(8,128)(2,1)S(1)}, u32[]{:S(2)}, u32[]{:S(2)}) %collective-permute-start.21) | collective-permute-done | bytes 98336 | tf_op jit(solution)/shard_map/ppermute | solution.py:43
  57.6 0.1 collective-permute-start.22
  57.7 2.4 %collective-permute-start.23 = (bf16[768,128]{1,0:T(8,128)(2,1)S(1)}, bf16[768,128]{1,0:T(8,128)(2,1)S(1)}, u32[]{:S(2)}, u32[]{:S(2)}) collective-permute-start(bf16[768,128]{1,0:T(8,128)(2,1)S(1)} %get-tuple-element.46), channel_id=1, source_target_pairs={{0,32},{8,40},{16,48},{24,56},{32,0},{40,8},{48,16},{56,24},{64,96... | collective-permute-start | bytes 589832 | tf_op jit(solution)/shard_map/ppermute | solution.py:43
  60.1 2.0 %collective-permute-start.24 = (bf16[768,128]{1,0:T(8,128)(2,1)S(1)}, bf16[768,128]{1,0:T(8,128)(2,1)S(1)}, u32[]{:S(2)}, u32[]{:S(2)}) collective-permute-start(bf16[768,128]{1,0:T(8,128)(2,1)S(1)} %get-tuple-element.47), channel_id=1, source_target_pairs={{0,96},{8,104},{16,112},{24,120},{32,64},{40,72},{48,80},{56,88},{... | collective-permute-start | bytes 589832 | tf_op jit(solution)/shard_map/ppermute | solution.py:43
  62.1 2.2 %collective-permute-start.25 = (bf16[768,128]{1,0:T(8,128)(2,1)S(1)}, bf16[768,128]{1,0:T(8,128)(2,1)S(1)}, u32[]{:S(2)}, u32[]{:S(2)}) collective-permute-start(bf16[768,128]{1,0:T(8,128)(2,1)S(1)} %get-tuple-element.48), channel_id=1, source_target_pairs={{0,64},{8,72},{16,80},{24,88},{32,96},{40,104},{48,112},{56,120},{... | collective-permute-start | bytes 589832 | tf_op jit(solution)/shard_map/ppermute | solution.py:43
  64.3 9.2 %collective-permute-done.23 = bf16[768,128]{1,0:T(8,128)(2,1)S(1)} collective-permute-done((bf16[768,128]{1,0:T(8,128)(2,1)S(1)}, bf16[768,128]{1,0:T(8,128)(2,1)S(1)}, u32[]{:S(2)}, u32[]{:S(2)}) %collective-permute-start.23) | collective-permute-done | bytes 196640 | tf_op jit(solution)/shard_map/ppermute | solution.py:43
  73.6 8.0 %collective-permute-done.24 = bf16[768,128]{1,0:T(8,128)(2,1)S(1)} collective-permute-done((bf16[768,128]{1,0:T(8,128)(2,1)S(1)}, bf16[768,128]{1,0:T(8,128)(2,1)S(1)}, u32[]{:S(2)}, u32[]{:S(2)}) %collective-permute-start.24) | collective-permute-done | bytes 196640 | tf_op jit(solution)/shard_map/ppermute | solution.py:43
  81.5 0.1 add_convert_fusion
  81.7 0.1 collective-permute-start.26
  81.8 14.7 %all_to_all.5 = bf16[8,24,256]{2,1,0:T(8,128)(2,1)S(1)} all-to-all(bf16[8,24,256]{2,1,0:T(8,128)(2,1)S(1)} %bitcast.28), channel_id=1, replica_groups=mesh['seq'=32,'head'=8] {'head'}, dimensions={0} | all-to-all | bytes 196608 | tf_op jit(solution)/shard_map/all_to_all | solution.py:309
  96.5 0.6 copy.9
  97.2 0.7 fusion.4
  (29 shorter events, 0.2 us)
Async XLA Ops:
  2.4 11.0 %collective-permute-start.1 = (bf16[400,256]{1,0:T(8,128)(2,1)S(1)}, bf16[400,256]{1,0:T(8,128)(2,1)S(1)}, u32[]{:S(2)}, u32[]{:S(2)}) collective-permute-start(bf16[400,256]{1,0:T(8,128)(2,1)S(1)} %get-tuple-element.56.refs_0_), channel_id=1, source_target_pairs={{0,16},{8,24},{16,0},{24,8},{32,48},{40,56},{48,32},{56,40},{64,80... | collective-permute-start | bytes 614408 | tf_op jit(solution)/shard_map/ppermute | solution.py:43
  4.3 15.3 %collective-permute-start.8 = (bf16[400,256]{1,0:T(8,128)(2,1)S(1)}, bf16[400,256]{1,0:T(8,128)(2,1)S(1)}, u32[]{:S(2)}, u32[]{:S(2)}) collective-permute-start(bf16[400,256]{1,0:T(8,128)(2,1)S(1)} %get-tuple-element.55.refs_8_), channel_id=1, source_target_pairs={{0,32},{8,40},{16,48},{24,56},{32,0},{40,8},{48,16},{56,24},{64,96... | collective-permute-start | bytes 614408 | tf_op jit(solution)/shard_map/ppermute | solution.py:43
  5.9 15.2 %collective-permute-start.10 = (bf16[400,256]{1,0:T(8,128)(2,1)S(1)}, bf16[400,256]{1,0:T(8,128)(2,1)S(1)}, u32[]{:S(2)}, u32[]{:S(2)}) collective-permute-start(bf16[400,256]{1,0:T(8,128)(2,1)S(1)} %get-tuple-element.55.refs_8_), channel_id=1, source_target_pairs={{0,96},{8,104},{16,112},{24,120},{32,64},{40,72},{48,80},{56,88},{... | collective-permute-start | bytes 614408 | tf_op jit(solution)/shard_map/ppermute | solution.py:43
  10.4 13.3 %collective-permute-start.3 = (bf16[400,256]{1,0:T(8,128)(2,1)S(1)}, bf16[400,256]{1,0:T(8,128)(2,1)S(1)}, u32[]{:S(2)}, u32[]{:S(2)}) collective-permute-start(bf16[400,256]{1,0:T(8,128)(2,1)S(1)} %get-tuple-element.56.refs_0_), channel_id=1, source_target_pairs={{0,128},{8,136},{16,144},{24,152},{32,160},{40,168},{48,176},{56,1... | collective-permute-start | bytes 614408 | tf_op jit(solution)/shard_map/ppermute | solution.py:43
  11.9 15.3 %collective-permute-start = (bf16[400,256]{1,0:T(8,128)(2,1)S(1)}, bf16[400,256]{1,0:T(8,128)(2,1)S(1)}, u32[]{:S(2)}, u32[]{:S(2)}) collective-permute-start(bf16[400,256]{1,0:T(8,128)(2,1)S(1)} %get-tuple-element.56.refs_0_), channel_id=1, source_target_pairs={{0,8},{8,0},{16,24},{24,16},{32,40},{40,32},{48,56},{56,48},{64,72... | collective-permute-start | bytes 614408 | tf_op jit(solution)/shard_map/ppermute | solution.py:43
  13.4 13.7 %collective-permute-start.7 = (bf16[400,256]{1,0:T(8,128)(2,1)S(1)}, bf16[400,256]{1,0:T(8,128)(2,1)S(1)}, u32[]{:S(2)}, u32[]{:S(2)}) collective-permute-start(bf16[400,256]{1,0:T(8,128)(2,1)S(1)} %get-tuple-element.55.refs_8_), channel_id=1, source_target_pairs={{0,8},{8,0},{16,24},{24,16},{32,40},{40,32},{48,56},{56,48},{64,72... | collective-permute-start | bytes 614408 | tf_op jit(solution)/shard_map/ppermute | solution.py:43
  19.6 8.7 %collective-permute-start.5 = (bf16[400,256]{1,0:T(8,128)(2,1)S(1)}, bf16[400,256]{1,0:T(8,128)(2,1)S(1)}, u32[]{:S(2)}, u32[]{:S(2)}) collective-permute-start(bf16[400,256]{1,0:T(8,128)(2,1)S(1)} %collective-permute-done.1.refs_2_), channel_id=1, source_target_pairs={{0,128},{8,136},{16,144},{24,152},{32,160},{40,168},{48,176},{56,1... | collective-permute-start | bytes 614408 | tf_op jit(solution)/shard_map/ppermute | solution.py:43
  21.2 7.2 %collective-permute-start.13 = (bf16[192,256]{1,0:T(8,128)(2,1)S(1)}, bf16[192,256]{1,0:T(8,128)(2,1)S(1)}, u32[]{:S(2)}, u32[]{:S(2)}) collective-permute-start(bf16[192,256]{1,0:T(8,128)(2,1)S(1)} %slice.9), channel_id=1, source_target_pairs={{0,96},{8,104},{16,112},{24,120},{32,64},{40,72},{48,80},{56,88},{... | collective-permute-start | bytes 294920 | tf_op jit(solution)/shard_map/ppermute | solution.py:43
  23.7 6.1 %collective-permute-start.12 = (bf16[208,256]{1,0:T(8,128)(2,1)S(1)}, bf16[208,256]{1,0:T(8,128)(2,1)S(1)}, u32[]{:S(2)}, u32[]{:S(2)}) collective-permute-start(bf16[208,256]{1,0:T(8,128)(2,1)S(1)} %slice.8), channel_id=1, source_target_pairs={{0,32},{8,40},{16,48},{24,56},{32,0},{40,8},{48,16},{56,24},{64,96... | collective-permute-start | bytes 319496 | tf_op jit(solution)/shard_map/ppermute | solution.py:43
  27.1 2.8 %collective-permute-start.2 = (bf16[400,256]{1,0:T(8,128)(2,1)S(1)}, bf16[400,256]{1,0:T(8,128)(2,1)S(1)}, u32[]{:S(2)}, u32[]{:S(2)}) collective-permute-start(bf16[400,256]{1,0:T(8,128)(2,1)S(1)} %collective-permute-done.1.refs_2_), channel_id=1, source_target_pairs={{0,8},{8,0},{16,24},{24,16},{32,40},{40,32},{48,56},{56,48},{64,72... | collective-permute-start | bytes 614408 | tf_op jit(solution)/shard_map/ppermute | solution.py:43
  27.1 3.3 %collective-permute-start.9 = (bf16[400,256]{1,0:T(8,128)(2,1)S(1)}, bf16[400,256]{1,0:T(8,128)(2,1)S(1)}, u32[]{:S(2)}, u32[]{:S(2)}) collective-permute-start(bf16[400,256]{1,0:T(8,128)(2,1)S(1)} %collective-permute-done.8.refs_10_), channel_id=1, source_target_pairs={{0,8},{8,0},{16,24},{24,16},{32,40},{40,32},{48,56},{56,48},{64,72... | collective-permute-start | bytes 614408 | tf_op jit(solution)/shard_map/ppermute | solution.py:43
  28.4 2.2 %collective-permute-start.4 = (bf16[400,256]{1,0:T(8,128)(2,1)S(1)}, bf16[400,256]{1,0:T(8,128)(2,1)S(1)}, u32[]{:S(2)}, u32[]{:S(2)}) collective-permute-start(bf16[400,256]{1,0:T(8,128)(2,1)S(1)} %collective-permute-done.3.refs_4_), channel_id=1, source_target_pairs={{0,8},{8,0},{16,24},{24,16},{32,40},{40,32},{48,56},{56,48},{64,72... | collective-permute-start | bytes 614408 | tf_op jit(solution)/shard_map/ppermute | solution.py:43
  28.4 2.2 %collective-permute-start.6 = (bf16[400,256]{1,0:T(8,128)(2,1)S(1)}, bf16[400,256]{1,0:T(8,128)(2,1)S(1)}, u32[]{:S(2)}, u32[]{:S(2)}) collective-permute-start(bf16[400,256]{1,0:T(8,128)(2,1)S(1)} %collective-permute-done.5.refs_6_), channel_id=1, source_target_pairs={{0,8},{8,0},{16,24},{24,16},{32,40},{40,32},{48,56},{56,48},{64,72... | collective-permute-start | bytes 614408 | tf_op jit(solution)/shard_map/ppermute | solution.py:43
  29.8 3.8 %collective-permute-start.11 = (bf16[400,256]{1,0:T(8,128)(2,1)S(1)}, bf16[400,256]{1,0:T(8,128)(2,1)S(1)}, u32[]{:S(2)}, u32[]{:S(2)}) collective-permute-start(bf16[400,256]{1,0:T(8,128)(2,1)S(1)} %collective-permute-done.10.refs_4_), channel_id=1, source_target_pairs={{0,8},{8,0},{16,24},{24,16},{32,40},{40,32},{48,56},{56,48},{64,72... | collective-permute-start | bytes 614408 | tf_op jit(solution)/shard_map/ppermute | solution.py:43
  29.9 5.5 %collective-permute-start.15 = (bf16[192,256]{1,0:T(8,128)(2,1)S(1)}, bf16[192,256]{1,0:T(8,128)(2,1)S(1)}, u32[]{:S(2)}, u32[]{:S(2)}) collective-permute-start(bf16[192,256]{1,0:T(8,128)(2,1)S(1)} %collective-permute-done.13.refs_5_), channel_id=1, source_target_pairs={{0,8},{8,0},{16,24},{24,16},{32,40},{40,32},{48,56},{56,48},{64,72... | collective-permute-start | bytes 294920 | tf_op jit(solution)/shard_map/ppermute | solution.py:43
  30.4 5.0 %collective-permute-start.14 = (bf16[208,256]{1,0:T(8,128)(2,1)S(1)}, bf16[208,256]{1,0:T(8,128)(2,1)S(1)}, u32[]{:S(2)}, u32[]{:S(2)}) collective-permute-start(bf16[208,256]{1,0:T(8,128)(2,1)S(1)} %collective-permute-done.12.refs_4_), channel_id=1, source_target_pairs={{0,8},{8,0},{16,24},{24,16},{32,40},{40,32},{48,56},{56,48},{64,72... | collective-permute-start | bytes 319496 | tf_op jit(solution)/shard_map/ppermute | solution.py:43
  37.3 5.0 %collective-permute-start.16 = (f32[8,1536]{1,0:T(8,128)S(1)}, f32[8,1536]{1,0:T(8,128)S(1)}, u32[]{:S(2)}, u32[]{:S(2)}) collective-permute-start(f32[8,1536]{1,0:T(8,128)S(1)} %get-tuple-element.40.refs_11_), channel_id=1, source_target_pairs={{0,16},{8,24},{16,0},{24,8},{32,48},{40,56},{48,32},{56,40},{64,80... | collective-permute-start | bytes 147464 | tf_op jit(solution)/shard_map/ppermute | solution.py:43
  40.0 4.6 %collective-permute-start.17 = (f32[8,1536]{1,0:T(8,128)S(1)}, f32[8,1536]{1,0:T(8,128)S(1)}, u32[]{:S(2)}, u32[]{:S(2)}) collective-permute-start(f32[8,1536]{1,0:T(8,128)S(1)} %get-tuple-element.40.refs_11_), channel_id=1, source_target_pairs={{0,128},{8,136},{16,144},{24,152},{32,160},{40,168},{48,176},{56,1... | collective-permute-start | bytes 147464 | tf_op jit(solution)/shard_map/ppermute | solution.py:43
  40.6 5.0 %collective-permute-start.18 = (f32[8,1536]{1,0:T(8,128)S(1)}, f32[8,1536]{1,0:T(8,128)S(1)}, u32[]{:S(2)}, u32[]{:S(2)}) collective-permute-start(f32[8,1536]{1,0:T(8,128)S(1)} %get-tuple-element.40.refs_11_), channel_id=1, source_target_pairs={{0,144},{8,152},{16,128},{24,136},{32,176},{40,184},{48,160},{56,1... | collective-permute-start | bytes 147464 | tf_op jit(solution)/shard_map/ppermute | solution.py:43
  50.3 4.9 %collective-permute-start.19 = (bf16[384,128]{1,0:T(8,128)(2,1)S(1)}, bf16[384,128]{1,0:T(8,128)(2,1)S(1)}, u32[]{:S(2)}, u32[]{:S(2)}) collective-permute-start(bf16[384,128]{1,0:T(8,128)(2,1)S(1)} %get-tuple-element.42), channel_id=1, source_target_pairs={{0,16},{8,24},{16,0},{24,8},{32,48},{40,56},{48,32},{56,40},{64,80... | collective-permute-start | bytes 294920 | tf_op jit(solution)/shard_map/ppermute | solution.py:43
  50.6 5.4 %collective-permute-start.20 = (bf16[384,128]{1,0:T(8,128)(2,1)S(1)}, bf16[384,128]{1,0:T(8,128)(2,1)S(1)}, u32[]{:S(2)}, u32[]{:S(2)}) collective-permute-start(bf16[384,128]{1,0:T(8,128)(2,1)S(1)} %get-tuple-element.43), channel_id=1, source_target_pairs={{0,128},{8,136},{16,144},{24,152},{32,160},{40,168},{48,176},{56,1... | collective-permute-start | bytes 294920 | tf_op jit(solution)/shard_map/ppermute | solution.py:43
  52.0 5.5 %collective-permute-start.21 = (bf16[384,128]{1,0:T(8,128)(2,1)S(1)}, bf16[384,128]{1,0:T(8,128)(2,1)S(1)}, u32[]{:S(2)}, u32[]{:S(2)}) collective-permute-start(bf16[384,128]{1,0:T(8,128)(2,1)S(1)} %get-tuple-element.44), channel_id=1, source_target_pairs={{0,144},{8,152},{16,128},{24,136},{32,176},{40,184},{48,160},{56,1... | collective-permute-start | bytes 294920 | tf_op jit(solution)/shard_map/ppermute | solution.py:43
  57.6 6.7 %collective-permute-start.22 = (bf16[192,128]{1,0:T(8,128)(2,1)S(1)}, bf16[192,128]{1,0:T(8,128)(2,1)S(1)}, u32[]{:S(2)}, u32[]{:S(2)}) collective-permute-start(bf16[192,128]{1,0:T(8,128)(2,1)S(1)} %dynamic-slice_bitcast_fusion.1), channel_id=1, source_target_pairs={{0,8},{8,0},{16,24},{24,16},{32,40},{40,32},{48,56},{56,48},{64,72... | collective-permute-start | bytes 147464 | tf_op jit(solution)/shard_map/ppermute | solution.py:43
  57.7 15.8 %collective-permute-start.23 = (bf16[768,128]{1,0:T(8,128)(2,1)S(1)}, bf16[768,128]{1,0:T(8,128)(2,1)S(1)}, u32[]{:S(2)}, u32[]{:S(2)}) collective-permute-start(bf16[768,128]{1,0:T(8,128)(2,1)S(1)} %get-tuple-element.46), channel_id=1, source_target_pairs={{0,32},{8,40},{16,48},{24,56},{32,0},{40,8},{48,16},{56,24},{64,96... | collective-permute-start | bytes 589832 | tf_op jit(solution)/shard_map/ppermute | solution.py:43
  60.1 21.4 %collective-permute-start.24 = (bf16[768,128]{1,0:T(8,128)(2,1)S(1)}, bf16[768,128]{1,0:T(8,128)(2,1)S(1)}, u32[]{:S(2)}, u32[]{:S(2)}) collective-permute-start(bf16[768,128]{1,0:T(8,128)(2,1)S(1)} %get-tuple-element.47), channel_id=1, source_target_pairs={{0,96},{8,104},{16,112},{24,120},{32,64},{40,72},{48,80},{56,88},{... | collective-permute-start | bytes 589832 | tf_op jit(solution)/shard_map/ppermute | solution.py:43
  62.1 19.4 %collective-permute-start.25 = (bf16[768,128]{1,0:T(8,128)(2,1)S(1)}, bf16[768,128]{1,0:T(8,128)(2,1)S(1)}, u32[]{:S(2)}, u32[]{:S(2)}) collective-permute-start(bf16[768,128]{1,0:T(8,128)(2,1)S(1)} %get-tuple-element.48), channel_id=1, source_target_pairs={{0,64},{8,72},{16,80},{24,88},{32,96},{40,104},{48,112},{56,120},{... | collective-permute-start | bytes 589832 | tf_op jit(solution)/shard_map/ppermute | solution.py:43
  81.7 15.5 %collective-permute-start.26 = (bf16[2,192,128]{2,1,0:T(8,128)(2,1)S(1)}, bf16[2,192,128]{2,1,0:T(8,128)(2,1)S(1)}, u32[]{:S(2)}, u32[]{:S(2)}) collective-permute-start(bf16[2,192,128]{2,1,0:T(8,128)(2,1)S(1)} %dynamic-slice_bitcast_fusion), channel_id=1, source_target_pairs={{0,8},{8,0},{16,24},{24,16},{32,40},{40,32},{48,56},{56,48},{64,72... | collective-permute-start | bytes 294920 | tf_op jit(solution)/shard_map/ppermute | solution.py:43

commit v2 on v1

--- a/solution.py
+++ b/solution.py
@@ -126,7 +126,7 @@
 
     def turn(i, running):
         top, total, delta = running
-        start = pl.multiple_of(i * tile, tile)
+        start = i * tile
         s = masked_scores(queries, keys, query_pos, key_pos, start, tile)
         g = dot_t(values[pl.ds(start, tile), :], grads[...])
         scores[pl.ds(start, tile), :] = s.reshape(tile, QUERIES)
@@ -139,7 +139,9 @@
         delta = delta * shrink + jnp.sum(p * g, axis=0)
         return new, total, delta
 
-    return lax.fori_loop(0, keys.shape[0] // tile, turn, running)
+    for i in range(keys.shape[0] // tile):
+        running = turn(i, running)
+    return running
 
 
 def first_kernel(where_ref, *refs):

time: 98.1 us -> 97.2 us (level)
  transfers between devices with their start and end apart: 27 -> 27, of which waited for: 12 -> 12; matrix products, arithmetic and copies ran while one was open for 1% -> 1% of each run, Pallas kernels for 5% -> 4%
where the time goes in v2:
time: 97.2 us; the launch traced here: 97.1 us
  waiting for transfers between devices  34.2 us (35%)
  starting transfers between devices  33.3 us (34%)
  blocking collectives  14.8 us (15%)
  Pallas kernels  10.5 us (11%)
  other arithmetic  2.73 us (3%)
    ppermute x27, waiting for transfers between devices, move(): return lax.ppermute(value, 'seq', perm(**how))  34.2 us
    ppermute x27, starting transfers between devices, move(): return lax.ppermute(value, 'seq', perm(**how))  33.3 us
    all_to_all x1, blocking collectives, body(): regrouped = lax.all_to_all(grad_query.reshape(8, 24, 256), 'head', 0, 0)  14.8 us
    pallas_call x4, Pallas kernels, call(): pl.pallas_call(kernel, out_shape=tuple(outs), in_specs=[pl.BlockSpec(memo...  10.5 us
  transfers between devices with their start and end apart: 27, of which 12 were waited for; matrix products, arithmetic and copies ran while one was open for 1% of the time, Pallas kernels for 4%

profile of v2, /device:TPU:32, one launch (start us, length us, event | category | flops | bytes accessed | tf_op | source)
XLA Modules:
  0.0 97.1 jit_solution(11593611438867037952)
XLA Ops:
  0.6 0.7 fusion.9
  1.4 1.1 %fusion.1 = (bf16[400,256]{1,0:T(8,128)(2,1)S(1)}, bf16[400,256]{1,0:T(8,128)(2,1)S(1)}) fusion(bf16[16,256]{1,0:T(8,128)(2,1)S(1)} %broadcast_bitcast_fusion, bf16[192,256]{1,0:T(8,128)(2,1)} %param.7, bf16[192,256]{1,0:T(8,128)(2,1)} %param.6, bf16[192,256]{1,0:T(8,128)(2,1)} %param.8, bf16[192,256]{1,0:T(8,128)(2,1)} %param.5), kind=kLoop, calls=%fused_computation.4 | loop fusion | flops 1126400 | bytes 811008 | tf_op jit(solution)/shard_map/concatenate | solution.py:56
  2.4 1.9 %collective-permute-start.1 = (bf16[400,256]{1,0:T(8,128)(2,1)S(1)}, bf16[400,256]{1,0:T(8,128)(2,1)S(1)}, u32[]{:S(2)}, u32[]{:S(2)}) collective-permute-start(bf16[400,256]{1,0:T(8,128)(2,1)S(1)} %get-tuple-element.56.refs_0_), channel_id=1, source_target_pairs={{0,16},{8,24},{16,0},{24,8},{32,48},{40,56},{48,32},{56,40},{64,80... | collective-permute-start | bytes 614408 | tf_op jit(solution)/shard_map/ppermute | solution.py:43
  4.3 1.6 %collective-permute-start.8 = (bf16[400,256]{1,0:T(8,128)(2,1)S(1)}, bf16[400,256]{1,0:T(8,128)(2,1)S(1)}, u32[]{:S(2)}, u32[]{:S(2)}) collective-permute-start(bf16[400,256]{1,0:T(8,128)(2,1)S(1)} %get-tuple-element.55.refs_8_), channel_id=1, source_target_pairs={{0,32},{8,40},{16,48},{24,56},{32,0},{40,8},{48,16},{56,24},{64,96... | collective-permute-start | bytes 614408 | tf_op jit(solution)/shard_map/ppermute | solution.py:43
  5.9 4.5 %collective-permute-start.10 = (bf16[400,256]{1,0:T(8,128)(2,1)S(1)}, bf16[400,256]{1,0:T(8,128)(2,1)S(1)}, u32[]{:S(2)}, u32[]{:S(2)}) collective-permute-start(bf16[400,256]{1,0:T(8,128)(2,1)S(1)} %get-tuple-element.55.refs_8_), channel_id=1, source_target_pairs={{0,96},{8,104},{16,112},{24,120},{32,64},{40,72},{48,80},{56,88},{... | collective-permute-start | bytes 614408 | tf_op jit(solution)/shard_map/ppermute | solution.py:43
  10.4 1.5 %collective-permute-start.3 = (bf16[400,256]{1,0:T(8,128)(2,1)S(1)}, bf16[400,256]{1,0:T(8,128)(2,1)S(1)}, u32[]{:S(2)}, u32[]{:S(2)}) collective-permute-start(bf16[400,256]{1,0:T(8,128)(2,1)S(1)} %get-tuple-element.56.refs_0_), channel_id=1, source_target_pairs={{0,128},{8,136},{16,144},{24,152},{32,160},{40,168},{48,176},{56,1... | collective-permute-start | bytes 614408 | tf_op jit(solution)/shard_map/ppermute | solution.py:43
  11.9 0.0 collective-permute-start
  11.9 1.5 %collective-permute-done.1.refs_2_ = bf16[400,256]{1,0:T(8,128)(2,1)S(1)} collective-permute-done((bf16[400,256]{1,0:T(8,128)(2,1)S(1)}, bf16[400,256]{1,0:T(8,128)(2,1)S(1)}, u32[]{:S(2)}, u32[]{:S(2)}) %collective-permute-start.1) | collective-permute-done | bytes 204832 | tf_op jit(solution)/shard_map/ppermute | solution.py:43
  13.4 0.0 collective-permute-start.7
  13.4 6.3 %collective-permute-done.8.refs_10_ = bf16[400,256]{1,0:T(8,128)(2,1)S(1)} collective-permute-done((bf16[400,256]{1,0:T(8,128)(2,1)S(1)}, bf16[400,256]{1,0:T(8,128)(2,1)S(1)}, u32[]{:S(2)}, u32[]{:S(2)}) %collective-permute-start.8) | collective-permute-done | bytes 204832 | tf_op jit(solution)/shard_map/ppermute | solution.py:43
  19.6 1.5 %collective-permute-start.5 = (bf16[400,256]{1,0:T(8,128)(2,1)S(1)}, bf16[400,256]{1,0:T(8,128)(2,1)S(1)}, u32[]{:S(2)}, u32[]{:S(2)}) collective-permute-start(bf16[400,256]{1,0:T(8,128)(2,1)S(1)} %collective-permute-done.1.refs_2_), channel_id=1, source_target_pairs={{0,128},{8,136},{16,144},{24,152},{32,160},{40,168},{48,176},{56,1... | collective-permute-start | bytes 614408 | tf_op jit(solution)/shard_map/ppermute | solution.py:43
  21.1 0.0 collective-permute-done.10.refs_4_
  21.2 2.5 %collective-permute-start.13 = (bf16[192,256]{1,0:T(8,128)(2,1)S(1)}, bf16[192,256]{1,0:T(8,128)(2,1)S(1)}, u32[]{:S(2)}, u32[]{:S(2)}) collective-permute-start(bf16[192,256]{1,0:T(8,128)(2,1)S(1)} %slice.9), channel_id=1, source_target_pairs={{0,96},{8,104},{16,112},{24,120},{32,64},{40,72},{48,80},{56,88},{... | collective-permute-start | bytes 294920 | tf_op jit(solution)/shard_map/ppermute | solution.py:43
  23.7 3.4 %collective-permute-start.12 = (bf16[208,256]{1,0:T(8,128)(2,1)S(1)}, bf16[208,256]{1,0:T(8,128)(2,1)S(1)}, u32[]{:S(2)}, u32[]{:S(2)}) collective-permute-start(bf16[208,256]{1,0:T(8,128)(2,1)S(1)} %slice.8), channel_id=1, source_target_pairs={{0,32},{8,40},{16,48},{24,56},{32,0},{40,8},{48,16},{56,24},{64,96... | collective-permute-start | bytes 319496 | tf_op jit(solution)/shard_map/ppermute | solution.py:43
  27.1 0.5 collective-permute-start.9
  27.6 0.7 collective-permute-done.13.refs_5_
  28.4 0.5 collective-permute-start.6
  28.9 1.0 collective-permute-done.12.refs_4_
  29.8 0.1 pad_add_fusion.where_ref
  29.9 0.5 collective-permute-start.15
  30.4 0.3 collective-permute-start.14
  30.7 2.8 %shard_map.76 = (bf16[1536,128]{1,0:T(8,128)(2,1)S(1)}, bf16[1536,128]{1,0:T(8,128)(2,1)S(1)}, f32[8,1536]{1,0:T(8,128)S(1)}, bf16[768,128]{1,0:T(8,128)(2,1)S(1...) custom-call(s32[2]{0:T(128)S(1)} %pad_add_fusion.where_ref, ...), custom_call_target="tpu_custom_call" | custom-call | flops 2000000000 | bytes 4000000 | tf_op jit(solution)/shard_map/pallas_call | solution.py:241
  33.5 1.5 %shard_map.77 = (bf16[384,128]{1,0:T(8,128)(2,1)S(1)}, f32[384,1536]{1,0:T(8,128)S(1)}, f32[384,1536]{1,0:T(8,128)S(1)}, f32[3,8,1536]{2,1,0:T(8,128)S(1)}) custom-call(s32[2]{0:T(128)S(1)} %pad_add_fusion.where_ref, bf16[1536,128]{1,0:T(8,128)(2,1)S(1)} %get-tuple-element.26.refs_0_, bf16[1536,128]{1,0:T(8,128)(2,1)S(1)} %get-tuple-element.27.refs_1_, ...), custom_call_target="tpu_custom_call" | custom-call | flops 1000000000 | bytes 4000000 | tf_op jit(solution)/shard_map/pallas_call | solution.py:241
  35.1 1.6 %shard_map.78 = (bf16[384,128]{1,0:T(8,128)(2,1)S(1)}, f32[384,1536]{1,0:T(8,128)S(1)}, f32[384,1536]{1,0:T(8,128)S(1)}, f32[8,1536]{1,0:T(8,128)S(1)}) custom-call(s32[2]{0:T(128)S(1)} %pad_add_fusion.where_ref, bf16[1536,128]{1,0:T(8,128)(2,1)S(1)} %get-tuple-element.26.refs_0_, bf16[1536,128]{1,0:T(8,128)(2,1)S(1)} %get-tuple-element.27.refs_1_, ...), custom_call_target="tpu_custom_call" | custom-call | flops 1000000000 | bytes 4000000 | tf_op jit(solution)/shard_map/pallas_call | solution.py:241
  36.6 2.7 %collective-permute-start.16 = (f32[8,1536]{1,0:T(8,128)S(1)}, f32[8,1536]{1,0:T(8,128)S(1)}, u32[]{:S(2)}, u32[]{:S(2)}) collective-permute-start(f32[8,1536]{1,0:T(8,128)S(1)} %get-tuple-element.40.refs_11_), channel_id=1, source_target_pairs={{0,16},{8,24},{16,0},{24,8},{32,48},{40,56},{48,32},{56,40},{64,80... | collective-permute-start | bytes 147464 | tf_op jit(solution)/shard_map/ppermute | solution.py:43
  39.3 0.5 collective-permute-start.17
  39.9 1.0 %collective-permute-start.18 = (f32[8,1536]{1,0:T(8,128)S(1)}, f32[8,1536]{1,0:T(8,128)S(1)}, u32[]{:S(2)}, u32[]{:S(2)}) collective-permute-start(f32[8,1536]{1,0:T(8,128)S(1)} %get-tuple-element.40.refs_11_), channel_id=1, source_target_pairs={{0,144},{8,152},{16,128},{24,136},{32,176},{40,184},{48,160},{56,1... | collective-permute-start | bytes 147464 | tf_op jit(solution)/shard_map/ppermute | solution.py:43
  40.9 0.6 collective-permute-done.16.refs_12_
  41.4 2.5 %collective-permute-done.17.refs_13_ = f32[8,1536]{1,0:T(8,128)S(1)} collective-permute-done((f32[8,1536]{1,0:T(8,128)S(1)}, f32[8,1536]{1,0:T(8,128)S(1)}, u32[]{:S(2)}, u32[]{:S(2)}) %collective-permute-start.17) | collective-permute-done | bytes 49184 | tf_op jit(solution)/shard_map/ppermute | solution.py:43
  43.9 0.9 collective-permute-done.18.refs_14_
  44.8 4.7 %shard_map.79 = (f32[384,128]{1,0:T(8,128)S(1)}, bf16[384,128]{1,0:T(8,128)(2,1)S(1)}, bf16[384,128]{1,0:T(8,128)(2,1)S(1)}, bf16[384,128]{1,0:T(8,128)(2,1)S(1)...) custom-call(s32[2]{0:T(128)S(1)} %pad_add_fusion.where_ref, ...), custom_call_target="tpu_custom_call" | custom-call | flops 6000000000 | bytes 4000000 | tf_op jit(solution)/shard_map/pallas_call | solution.py:241
  49.5 0.2 collective-permute-start.19
  49.7 1.5 %collective-permute-start.20 = (bf16[384,128]{1,0:T(8,128)(2,1)S(1)}, bf16[384,128]{1,0:T(8,128)(2,1)S(1)}, u32[]{:S(2)}, u32[]{:S(2)}) collective-permute-start(bf16[384,128]{1,0:T(8,128)(2,1)S(1)} %get-tuple-element.43), channel_id=1, source_target_pairs={{0,128},{8,136},{16,144},{24,152},{32,160},{40,168},{48,176},{56,1... | collective-permute-start | bytes 294920 | tf_op jit(solution)/shard_map/ppermute | solution.py:43
  51.2 1.9 %collective-permute-start.21 = (bf16[384,128]{1,0:T(8,128)(2,1)S(1)}, bf16[384,128]{1,0:T(8,128)(2,1)S(1)}, u32[]{:S(2)}, u32[]{:S(2)}) collective-permute-start(bf16[384,128]{1,0:T(8,128)(2,1)S(1)} %get-tuple-element.44), channel_id=1, source_target_pairs={{0,144},{8,152},{16,128},{24,136},{32,176},{40,184},{48,160},{56,1... | collective-permute-start | bytes 294920 | tf_op jit(solution)/shard_map/ppermute | solution.py:43
  53.1 1.1 %collective-permute-done.19 = bf16[384,128]{1,0:T(8,128)(2,1)S(1)} collective-permute-done((bf16[384,128]{1,0:T(8,128)(2,1)S(1)}, bf16[384,128]{1,0:T(8,128)(2,1)S(1)}, u32[]{:S(2)}, u32[]{:S(2)}) %collective-permute-start.19) | collective-permute-done | bytes 98336 | tf_op jit(solution)/shard_map/ppermute | solution.py:43
  54.2 0.8 collective-permute-done.20
  55.0 1.7 %collective-permute-done.21 = bf16[384,128]{1,0:T(8,128)(2,1)S(1)} collective-permute-done((bf16[384,128]{1,0:T(8,128)(2,1)S(1)}, bf16[384,128]{1,0:T(8,128)(2,1)S(1)}, u32[]{:S(2)}, u32[]{:S(2)}) %collective-permute-start.21) | collective-permute-done | bytes 98336 | tf_op jit(solution)/shard_map/ppermute | solution.py:43
  56.8 0.1 collective-permute-start.22
  56.9 2.6 %collective-permute-start.23 = (bf16[768,128]{1,0:T(8,128)(2,1)S(1)}, bf16[768,128]{1,0:T(8,128)(2,1)S(1)}, u32[]{:S(2)}, u32[]{:S(2)}) collective-permute-start(bf16[768,128]{1,0:T(8,128)(2,1)S(1)} %get-tuple-element.46), channel_id=1, source_target_pairs={{0,32},{8,40},{16,48},{24,56},{32,0},{40,8},{48,16},{56,24},{64,96... | collective-permute-start | bytes 589832 | tf_op jit(solution)/shard_map/ppermute | solution.py:43
  59.5 2.0 %collective-permute-start.24 = (bf16[768,128]{1,0:T(8,128)(2,1)S(1)}, bf16[768,128]{1,0:T(8,128)(2,1)S(1)}, u32[]{:S(2)}, u32[]{:S(2)}) collective-permute-start(bf16[768,128]{1,0:T(8,128)(2,1)S(1)} %get-tuple-element.47), channel_id=1, source_target_pairs={{0,96},{8,104},{16,112},{24,120},{32,64},{40,72},{48,80},{56,88},{... | collective-permute-start | bytes 589832 | tf_op jit(solution)/shard_map/ppermute | solution.py:43
  61.5 2.0 %collective-permute-start.25 = (bf16[768,128]{1,0:T(8,128)(2,1)S(1)}, bf16[768,128]{1,0:T(8,128)(2,1)S(1)}, u32[]{:S(2)}, u32[]{:S(2)}) collective-permute-start(bf16[768,128]{1,0:T(8,128)(2,1)S(1)} %get-tuple-element.48), channel_id=1, source_target_pairs={{0,64},{8,72},{16,80},{24,88},{32,96},{40,104},{48,112},{56,120},{... | collective-permute-start | bytes 589832 | tf_op jit(solution)/shard_map/ppermute | solution.py:43
  63.5 9.6 %collective-permute-done.23 = bf16[768,128]{1,0:T(8,128)(2,1)S(1)} collective-permute-done((bf16[768,128]{1,0:T(8,128)(2,1)S(1)}, bf16[768,128]{1,0:T(8,128)(2,1)S(1)}, u32[]{:S(2)}, u32[]{:S(2)}) %collective-permute-start.23) | collective-permute-done | bytes 196640 | tf_op jit(solution)/shard_map/ppermute | solution.py:43
  73.0 7.6 %collective-permute-done.24 = bf16[768,128]{1,0:T(8,128)(2,1)S(1)} collective-permute-done((bf16[768,128]{1,0:T(8,128)(2,1)S(1)}, bf16[768,128]{1,0:T(8,128)(2,1)S(1)}, u32[]{:S(2)}, u32[]{:S(2)}) %collective-permute-start.24) | collective-permute-done | bytes 196640 | tf_op jit(solution)/shard_map/ppermute | solution.py:43
  80.7 0.1 add_convert_fusion
  80.8 0.1 collective-permute-start.26
  80.9 14.8 %all_to_all.5 = bf16[8,24,256]{2,1,0:T(8,128)(2,1)S(1)} all-to-all(bf16[8,24,256]{2,1,0:T(8,128)(2,1)S(1)} %bitcast.28), channel_id=1, replica_groups=mesh['seq'=32,'head'=8] {'head'}, dimensions={0} | all-to-all | bytes 196608 | tf_op jit(solution)/shard_map/all_to_all | solution.py:311
  95.7 0.6 copy.9
  96.4 0.7 fusion.4
  (29 shorter events, 0.2 us)
Async XLA Ops:
  2.4 11.0 %collective-permute-start.1 = (bf16[400,256]{1,0:T(8,128)(2,1)S(1)}, bf16[400,256]{1,0:T(8,128)(2,1)S(1)}, u32[]{:S(2)}, u32[]{:S(2)}) collective-permute-start(bf16[400,256]{1,0:T(8,128)(2,1)S(1)} %get-tuple-element.56.refs_0_), channel_id=1, source_target_pairs={{0,16},{8,24},{16,0},{24,8},{32,48},{40,56},{48,32},{56,40},{64,80... | collective-permute-start | bytes 614408 | tf_op jit(solution)/shard_map/ppermute | solution.py:43
  4.3 15.3 %collective-permute-start.8 = (bf16[400,256]{1,0:T(8,128)(2,1)S(1)}, bf16[400,256]{1,0:T(8,128)(2,1)S(1)}, u32[]{:S(2)}, u32[]{:S(2)}) collective-permute-start(bf16[400,256]{1,0:T(8,128)(2,1)S(1)} %get-tuple-element.55.refs_8_), channel_id=1, source_target_pairs={{0,32},{8,40},{16,48},{24,56},{32,0},{40,8},{48,16},{56,24},{64,96... | collective-permute-start | bytes 614408 | tf_op jit(solution)/shard_map/ppermute | solution.py:43
  5.9 15.2 %collective-permute-start.10 = (bf16[400,256]{1,0:T(8,128)(2,1)S(1)}, bf16[400,256]{1,0:T(8,128)(2,1)S(1)}, u32[]{:S(2)}, u32[]{:S(2)}) collective-permute-start(bf16[400,256]{1,0:T(8,128)(2,1)S(1)} %get-tuple-element.55.refs_8_), channel_id=1, source_target_pairs={{0,96},{8,104},{16,112},{24,120},{32,64},{40,72},{48,80},{56,88},{... | collective-permute-start | bytes 614408 | tf_op jit(solution)/shard_map/ppermute | solution.py:43
  10.4 13.3 %collective-permute-start.3 = (bf16[400,256]{1,0:T(8,128)(2,1)S(1)}, bf16[400,256]{1,0:T(8,128)(2,1)S(1)}, u32[]{:S(2)}, u32[]{:S(2)}) collective-permute-start(bf16[400,256]{1,0:T(8,128)(2,1)S(1)} %get-tuple-element.56.refs_0_), channel_id=1, source_target_pairs={{0,128},{8,136},{16,144},{24,152},{32,160},{40,168},{48,176},{56,1... | collective-permute-start | bytes 614408 | tf_op jit(solution)/shard_map/ppermute | solution.py:43
  11.9 15.3 %collective-permute-start = (bf16[400,256]{1,0:T(8,128)(2,1)S(1)}, bf16[400,256]{1,0:T(8,128)(2,1)S(1)}, u32[]{:S(2)}, u32[]{:S(2)}) collective-permute-start(bf16[400,256]{1,0:T(8,128)(2,1)S(1)} %get-tuple-element.56.refs_0_), channel_id=1, source_target_pairs={{0,8},{8,0},{16,24},{24,16},{32,40},{40,32},{48,56},{56,48},{64,72... | collective-permute-start | bytes 614408 | tf_op jit(solution)/shard_map/ppermute | solution.py:43
  13.4 13.7 %collective-permute-start.7 = (bf16[400,256]{1,0:T(8,128)(2,1)S(1)}, bf16[400,256]{1,0:T(8,128)(2,1)S(1)}, u32[]{:S(2)}, u32[]{:S(2)}) collective-permute-start(bf16[400,256]{1,0:T(8,128)(2,1)S(1)} %get-tuple-element.55.refs_8_), channel_id=1, source_target_pairs={{0,8},{8,0},{16,24},{24,16},{32,40},{40,32},{48,56},{56,48},{64,72... | collective-permute-start | bytes 614408 | tf_op jit(solution)/shard_map/ppermute | solution.py:43
  19.6 8.7 %collective-permute-start.5 = (bf16[400,256]{1,0:T(8,128)(2,1)S(1)}, bf16[400,256]{1,0:T(8,128)(2,1)S(1)}, u32[]{:S(2)}, u32[]{:S(2)}) collective-permute-start(bf16[400,256]{1,0:T(8,128)(2,1)S(1)} %collective-permute-done.1.refs_2_), channel_id=1, source_target_pairs={{0,128},{8,136},{16,144},{24,152},{32,160},{40,168},{48,176},{56,1... | collective-permute-start | bytes 614408 | tf_op jit(solution)/shard_map/ppermute | solution.py:43
  21.2 7.2 %collective-permute-start.13 = (bf16[192,256]{1,0:T(8,128)(2,1)S(1)}, bf16[192,256]{1,0:T(8,128)(2,1)S(1)}, u32[]{:S(2)}, u32[]{:S(2)}) collective-permute-start(bf16[192,256]{1,0:T(8,128)(2,1)S(1)} %slice.9), channel_id=1, source_target_pairs={{0,96},{8,104},{16,112},{24,120},{32,64},{40,72},{48,80},{56,88},{... | collective-permute-start | bytes 294920 | tf_op jit(solution)/shard_map/ppermute | solution.py:43
  23.7 6.1 %collective-permute-start.12 = (bf16[208,256]{1,0:T(8,128)(2,1)S(1)}, bf16[208,256]{1,0:T(8,128)(2,1)S(1)}, u32[]{:S(2)}, u32[]{:S(2)}) collective-permute-start(bf16[208,256]{1,0:T(8,128)(2,1)S(1)} %slice.8), channel_id=1, source_target_pairs={{0,32},{8,40},{16,48},{24,56},{32,0},{40,8},{48,16},{56,24},{64,96... | collective-permute-start | bytes 319496 | tf_op jit(solution)/shard_map/ppermute | solution.py:43
  27.1 2.8 %collective-permute-start.2 = (bf16[400,256]{1,0:T(8,128)(2,1)S(1)}, bf16[400,256]{1,0:T(8,128)(2,1)S(1)}, u32[]{:S(2)}, u32[]{:S(2)}) collective-permute-start(bf16[400,256]{1,0:T(8,128)(2,1)S(1)} %collective-permute-done.1.refs_2_), channel_id=1, source_target_pairs={{0,8},{8,0},{16,24},{24,16},{32,40},{40,32},{48,56},{56,48},{64,72... | collective-permute-start | bytes 614408 | tf_op jit(solution)/shard_map/ppermute | solution.py:43
  27.1 3.3 %collective-permute-start.9 = (bf16[400,256]{1,0:T(8,128)(2,1)S(1)}, bf16[400,256]{1,0:T(8,128)(2,1)S(1)}, u32[]{:S(2)}, u32[]{:S(2)}) collective-permute-start(bf16[400,256]{1,0:T(8,128)(2,1)S(1)} %collective-permute-done.8.refs_10_), channel_id=1, source_target_pairs={{0,8},{8,0},{16,24},{24,16},{32,40},{40,32},{48,56},{56,48},{64,72... | collective-permute-start | bytes 614408 | tf_op jit(solution)/shard_map/ppermute | solution.py:43
  28.4 2.4 %collective-permute-start.4 = (bf16[400,256]{1,0:T(8,128)(2,1)S(1)}, bf16[400,256]{1,0:T(8,128)(2,1)S(1)}, u32[]{:S(2)}, u32[]{:S(2)}) collective-permute-start(bf16[400,256]{1,0:T(8,128)(2,1)S(1)} %collective-permute-done.3.refs_4_), channel_id=1, source_target_pairs={{0,8},{8,0},{16,24},{24,16},{32,40},{40,32},{48,56},{56,48},{64,72... | collective-permute-start | bytes 614408 | tf_op jit(solution)/shard_map/ppermute | solution.py:43
  28.4 2.4 %collective-permute-start.6 = (bf16[400,256]{1,0:T(8,128)(2,1)S(1)}, bf16[400,256]{1,0:T(8,128)(2,1)S(1)}, u32[]{:S(2)}, u32[]{:S(2)}) collective-permute-start(bf16[400,256]{1,0:T(8,128)(2,1)S(1)} %collective-permute-done.5.refs_6_), channel_id=1, source_target_pairs={{0,8},{8,0},{16,24},{24,16},{32,40},{40,32},{48,56},{56,48},{64,72... | collective-permute-start | bytes 614408 | tf_op jit(solution)/shard_map/ppermute | solution.py:43
  29.8 3.7 %collective-permute-start.11 = (bf16[400,256]{1,0:T(8,128)(2,1)S(1)}, bf16[400,256]{1,0:T(8,128)(2,1)S(1)}, u32[]{:S(2)}, u32[]{:S(2)}) collective-permute-start(bf16[400,256]{1,0:T(8,128)(2,1)S(1)} %collective-permute-done.10.refs_4_), channel_id=1, source_target_pairs={{0,8},{8,0},{16,24},{24,16},{32,40},{40,32},{48,56},{56,48},{64,72... | collective-permute-start | bytes 614408 | tf_op jit(solution)/shard_map/ppermute | solution.py:43
  29.9 5.1 %collective-permute-start.15 = (bf16[192,256]{1,0:T(8,128)(2,1)S(1)}, bf16[192,256]{1,0:T(8,128)(2,1)S(1)}, u32[]{:S(2)}, u32[]{:S(2)}) collective-permute-start(bf16[192,256]{1,0:T(8,128)(2,1)S(1)} %collective-permute-done.13.refs_5_), channel_id=1, source_target_pairs={{0,8},{8,0},{16,24},{24,16},{32,40},{40,32},{48,56},{56,48},{64,72... | collective-permute-start | bytes 294920 | tf_op jit(solution)/shard_map/ppermute | solution.py:43
  30.4 4.6 %collective-permute-start.14 = (bf16[208,256]{1,0:T(8,128)(2,1)S(1)}, bf16[208,256]{1,0:T(8,128)(2,1)S(1)}, u32[]{:S(2)}, u32[]{:S(2)}) collective-permute-start(bf16[208,256]{1,0:T(8,128)(2,1)S(1)} %collective-permute-done.12.refs_4_), channel_id=1, source_target_pairs={{0,8},{8,0},{16,24},{24,16},{32,40},{40,32},{48,56},{56,48},{64,72... | collective-permute-start | bytes 319496 | tf_op jit(solution)/shard_map/ppermute | solution.py:43
  36.6 4.8 %collective-permute-start.16 = (f32[8,1536]{1,0:T(8,128)S(1)}, f32[8,1536]{1,0:T(8,128)S(1)}, u32[]{:S(2)}, u32[]{:S(2)}) collective-permute-start(f32[8,1536]{1,0:T(8,128)S(1)} %get-tuple-element.40.refs_11_), channel_id=1, source_target_pairs={{0,16},{8,24},{16,0},{24,8},{32,48},{40,56},{48,32},{56,40},{64,80... | collective-permute-start | bytes 147464 | tf_op jit(solution)/shard_map/ppermute | solution.py:43
  39.3 4.6 %collective-permute-start.17 = (f32[8,1536]{1,0:T(8,128)S(1)}, f32[8,1536]{1,0:T(8,128)S(1)}, u32[]{:S(2)}, u32[]{:S(2)}) collective-permute-start(f32[8,1536]{1,0:T(8,128)S(1)} %get-tuple-element.40.refs_11_), channel_id=1, source_target_pairs={{0,128},{8,136},{16,144},{24,152},{32,160},{40,168},{48,176},{56,1... | collective-permute-start | bytes 147464 | tf_op jit(solution)/shard_map/ppermute | solution.py:43
  39.9 5.0 %collective-permute-start.18 = (f32[8,1536]{1,0:T(8,128)S(1)}, f32[8,1536]{1,0:T(8,128)S(1)}, u32[]{:S(2)}, u32[]{:S(2)}) collective-permute-start(f32[8,1536]{1,0:T(8,128)S(1)} %get-tuple-element.40.refs_11_), channel_id=1, source_target_pairs={{0,144},{8,152},{16,128},{24,136},{32,176},{40,184},{48,160},{56,1... | collective-permute-start | bytes 147464 | tf_op jit(solution)/shard_map/ppermute | solution.py:43
  49.5 4.7 %collective-permute-start.19 = (bf16[384,128]{1,0:T(8,128)(2,1)S(1)}, bf16[384,128]{1,0:T(8,128)(2,1)S(1)}, u32[]{:S(2)}, u32[]{:S(2)}) collective-permute-start(bf16[384,128]{1,0:T(8,128)(2,1)S(1)} %get-tuple-element.42), channel_id=1, source_target_pairs={{0,16},{8,24},{16,0},{24,8},{32,48},{40,56},{48,32},{56,40},{64,80... | collective-permute-start | bytes 294920 | tf_op jit(solution)/shard_map/ppermute | solution.py:43
  49.7 5.3 %collective-permute-start.20 = (bf16[384,128]{1,0:T(8,128)(2,1)S(1)}, bf16[384,128]{1,0:T(8,128)(2,1)S(1)}, u32[]{:S(2)}, u32[]{:S(2)}) collective-permute-start(bf16[384,128]{1,0:T(8,128)(2,1)S(1)} %get-tuple-element.43), channel_id=1, source_target_pairs={{0,128},{8,136},{16,144},{24,152},{32,160},{40,168},{48,176},{56,1... | collective-permute-start | bytes 294920 | tf_op jit(solution)/shard_map/ppermute | solution.py:43
  51.2 5.5 %collective-permute-start.21 = (bf16[384,128]{1,0:T(8,128)(2,1)S(1)}, bf16[384,128]{1,0:T(8,128)(2,1)S(1)}, u32[]{:S(2)}, u32[]{:S(2)}) collective-permute-start(bf16[384,128]{1,0:T(8,128)(2,1)S(1)} %get-tuple-element.44), channel_id=1, source_target_pairs={{0,144},{8,152},{16,128},{24,136},{32,176},{40,184},{48,160},{56,1... | collective-permute-start | bytes 294920 | tf_op jit(solution)/shard_map/ppermute | solution.py:43
  56.8 6.7 %collective-permute-start.22 = (bf16[192,128]{1,0:T(8,128)(2,1)S(1)}, bf16[192,128]{1,0:T(8,128)(2,1)S(1)}, u32[]{:S(2)}, u32[]{:S(2)}) collective-permute-start(bf16[192,128]{1,0:T(8,128)(2,1)S(1)} %dynamic-slice_bitcast_fusion.1), channel_id=1, source_target_pairs={{0,8},{8,0},{16,24},{24,16},{32,40},{40,32},{48,56},{56,48},{64,72... | collective-permute-start | bytes 147464 | tf_op jit(solution)/shard_map/ppermute | solution.py:43
  56.9 16.2 %collective-permute-start.23 = (bf16[768,128]{1,0:T(8,128)(2,1)S(1)}, bf16[768,128]{1,0:T(8,128)(2,1)S(1)}, u32[]{:S(2)}, u32[]{:S(2)}) collective-permute-start(bf16[768,128]{1,0:T(8,128)(2,1)S(1)} %get-tuple-element.46), channel_id=1, source_target_pairs={{0,32},{8,40},{16,48},{24,56},{32,0},{40,8},{48,16},{56,24},{64,96... | collective-permute-start | bytes 589832 | tf_op jit(solution)/shard_map/ppermute | solution.py:43
  59.5 21.2 %collective-permute-start.24 = (bf16[768,128]{1,0:T(8,128)(2,1)S(1)}, bf16[768,128]{1,0:T(8,128)(2,1)S(1)}, u32[]{:S(2)}, u32[]{:S(2)}) collective-permute-start(bf16[768,128]{1,0:T(8,128)(2,1)S(1)} %get-tuple-element.47), channel_id=1, source_target_pairs={{0,96},{8,104},{16,112},{24,120},{32,64},{40,72},{48,80},{56,88},{... | collective-permute-start | bytes 589832 | tf_op jit(solution)/shard_map/ppermute | solution.py:43
  61.5 19.2 %collective-permute-start.25 = (bf16[768,128]{1,0:T(8,128)(2,1)S(1)}, bf16[768,128]{1,0:T(8,128)(2,1)S(1)}, u32[]{:S(2)}, u32[]{:S(2)}) collective-permute-start(bf16[768,128]{1,0:T(8,128)(2,1)S(1)} %get-tuple-element.48), channel_id=1, source_target_pairs={{0,64},{8,72},{16,80},{24,88},{32,96},{40,104},{48,112},{56,120},{... | collective-permute-start | bytes 589832 | tf_op jit(solution)/shard_map/ppermute | solution.py:43
  80.8 15.5 %collective-permute-start.26 = (bf16[2,192,128]{2,1,0:T(8,128)(2,1)S(1)}, bf16[2,192,128]{2,1,0:T(8,128)(2,1)S(1)}, u32[]{:S(2)}, u32[]{:S(2)}) collective-permute-start(bf16[2,192,128]{2,1,0:T(8,128)(2,1)S(1)} %dynamic-slice_bitcast_fusion), channel_id=1, source_target_pairs={{0,8},{8,0},{16,24},{24,16},{32,40},{40,32},{48,56},{56,48},{64,72... | collective-permute-start | bytes 294920 | tf_op jit(solution)/shard_map/ppermute | solution.py:43

commit v3 on v2

--- a/solution.py
+++ b/solution.py
@@ -13,6 +13,7 @@
 BOTH = 2 * ROWS
 QUAD = 4
 QUERIES = QUAD * BOTH
+HALF = QUERIES // 2
 MID, LAST = 3, 2
 FIRST_MIB = 16
 GRADS_MIB = 16
@@ -174,10 +175,11 @@
         return
     best = jnp.max(top, axis=0, keepdims=True)
     shrink = jnp.exp2(top - best)
-    out[0:1, :] = best
-    out[1:2, :] = jnp.sum(total * shrink, axis=0, keepdims=True)
-    out[2:3, :] = jnp.sum(delta * shrink, axis=0, keepdims=True)
-    out[3:8, :] = jnp.zeros((5, QUERIES), F32)
+    sums = [jnp.sum(v * shrink, axis=0, keepdims=True) for v in (total, delta)]
+    for n, row in enumerate((best, *sums)):
+        for part in range(2):
+            out[2 * n + part : 2 * n + part + 1, :] = row[:, part * HALF : (part + 1) * HALF]
+    out[6:8, :] = jnp.zeros((2, HALF), F32)
 
 
 def grads_kernel(where_ref, *refs):
@@ -188,12 +190,12 @@
     own_keys, key_outs = refs[19], refs[20:23]
     query_sum, query_rows = refs[23:]
     mine = where_ref[0]
-    stats = [r[...] for r in stat_refs]
-    tops = [s[0:1] for s in stats]
+    stats = [[jnp.concatenate([r[2 * n : 2 * n + 1, :], r[2 * n + 1 : 2 * n + 2, :]], axis=1) for n in range(3)] for r in stat_refs]
+    tops = [s[0] for s in stats]
     best = functools.reduce(jnp.maximum, tops)
     shrinks = [jnp.exp2(t - best) for t in tops]
-    total = sum(s[1:2] * w for s, w in zip(stats, shrinks))
-    delta = sum(s[2:3] * w for s, w in zip(stats, shrinks)) / total
+    total = sum(s[1] * w for s, w in zip(stats, shrinks))
+    delta = sum(s[2] * w for s, w in zip(stats, shrinks)) / total
     log_total = jnp.broadcast_to(best + jnp.log2(total), (8, QUERIES))
     delta = jnp.broadcast_to(delta, (8, QUERIES))
     query_sum[...] = jnp.zeros_like(query_sum)
@@ -292,7 +294,7 @@
         *taken, found, *all_keys[4:6],
     )
     keys_b, scores_b, products_b, stats = call(
-        functools.partial(later_kernel, True), outs + [shaped(8, QUERIES, dtype=F32)], spare, 10**9, FIRST_MIB,
+        functools.partial(later_kernel, True), outs + [shaped(8, HALF, dtype=F32)], spare, 10**9, FIRST_MIB,
         where, *taken, found, *far_keys,
     )
     all_stats = [stats] + [near_move(stats, t) for t in range(1, QUAD)]

time: 97.2 us -> 96.7 us (level)
  no operation moved by 1% of the time
where the time goes in v3:
time: 96.7 us; the launch traced here: 96.6 us
  waiting for transfers between devices  34 us (35%)
  starting transfers between devices  33.4 us (35%)
  blocking collectives  14.7 us (15%)
  Pallas kernels  10.3 us (11%)
  other arithmetic  2.73 us (3%)
    ppermute x27, waiting for transfers between devices, move(): return lax.ppermute(value, 'seq', perm(**how))  34 us
    ppermute x27, starting transfers between devices, move(): return lax.ppermute(value, 'seq', perm(**how))  33.4 us
    all_to_all x1, blocking collectives, body(): regrouped = lax.all_to_all(grad_query.reshape(8, 24, 256), 'head', 0, 0)  14.7 us
    pallas_call x4, Pallas kernels, call(): pl.pallas_call(kernel, out_shape=tuple(outs), in_specs=[pl.BlockSpec(memo...  10.3 us
  transfers between devices with their start and end apart: 27, of which 12 were waited for; matrix products, arithmetic and copies ran while one was open for 1% of the time, Pallas kernels for 4%

profile of v3, /device:TPU:32, one launch (start us, length us, event | category | flops | bytes accessed | tf_op | source)
XLA Modules:
  0.0 96.6 jit_solution(9778852640553817271)
XLA Ops:
  0.6 0.7 fusion.9
  1.4 1.1 %fusion.1 = (bf16[400,256]{1,0:T(8,128)(2,1)S(1)}, bf16[400,256]{1,0:T(8,128)(2,1)S(1)}) fusion(bf16[16,256]{1,0:T(8,128)(2,1)S(1)} %broadcast_bitcast_fusion, bf16[192,256]{1,0:T(8,128)(2,1)} %param.7, bf16[192,256]{1,0:T(8,128)(2,1)} %param.6, bf16[192,256]{1,0:T(8,128)(2,1)} %param.8, bf16[192,256]{1,0:T(8,128)(2,1)} %param.5), kind=kLoop, calls=%fused_computation.4 | loop fusion | flops 1126400 | bytes 811008 | tf_op jit(solution)/shard_map/concatenate | solution.py:57
  2.4 1.9 %collective-permute-start.1 = (bf16[400,256]{1,0:T(8,128)(2,1)S(1)}, bf16[400,256]{1,0:T(8,128)(2,1)S(1)}, u32[]{:S(2)}, u32[]{:S(2)}) collective-permute-start(bf16[400,256]{1,0:T(8,128)(2,1)S(1)} %get-tuple-element.56.refs_0_), channel_id=1, source_target_pairs={{0,16},{8,24},{16,0},{24,8},{32,48},{40,56},{48,32},{56,40},{64,80... | collective-permute-start | bytes 614408 | tf_op jit(solution)/shard_map/ppermute | solution.py:44
  4.3 1.6 %collective-permute-start.8 = (bf16[400,256]{1,0:T(8,128)(2,1)S(1)}, bf16[400,256]{1,0:T(8,128)(2,1)S(1)}, u32[]{:S(2)}, u32[]{:S(2)}) collective-permute-start(bf16[400,256]{1,0:T(8,128)(2,1)S(1)} %get-tuple-element.55.refs_8_), channel_id=1, source_target_pairs={{0,32},{8,40},{16,48},{24,56},{32,0},{40,8},{48,16},{56,24},{64,96... | collective-permute-start | bytes 614408 | tf_op jit(solution)/shard_map/ppermute | solution.py:44
  5.9 4.5 %collective-permute-start.10 = (bf16[400,256]{1,0:T(8,128)(2,1)S(1)}, bf16[400,256]{1,0:T(8,128)(2,1)S(1)}, u32[]{:S(2)}, u32[]{:S(2)}) collective-permute-start(bf16[400,256]{1,0:T(8,128)(2,1)S(1)} %get-tuple-element.55.refs_8_), channel_id=1, source_target_pairs={{0,96},{8,104},{16,112},{24,120},{32,64},{40,72},{48,80},{56,88},{... | collective-permute-start | bytes 614408 | tf_op jit(solution)/shard_map/ppermute | solution.py:44
  10.4 1.5 %collective-permute-start.3 = (bf16[400,256]{1,0:T(8,128)(2,1)S(1)}, bf16[400,256]{1,0:T(8,128)(2,1)S(1)}, u32[]{:S(2)}, u32[]{:S(2)}) collective-permute-start(bf16[400,256]{1,0:T(8,128)(2,1)S(1)} %get-tuple-element.56.refs_0_), channel_id=1, source_target_pairs={{0,128},{8,136},{16,144},{24,152},{32,160},{40,168},{48,176},{56,1... | collective-permute-start | bytes 614408 | tf_op jit(solution)/shard_map/ppermute | solution.py:44
  11.9 0.0 collective-permute-start
  11.9 1.5 %collective-permute-done.1.refs_2_ = bf16[400,256]{1,0:T(8,128)(2,1)S(1)} collective-permute-done((bf16[400,256]{1,0:T(8,128)(2,1)S(1)}, bf16[400,256]{1,0:T(8,128)(2,1)S(1)}, u32[]{:S(2)}, u32[]{:S(2)}) %collective-permute-start.1) | collective-permute-done | bytes 204832 | tf_op jit(solution)/shard_map/ppermute | solution.py:44
  13.4 0.0 collective-permute-start.7
  13.4 6.3 %collective-permute-done.8.refs_10_ = bf16[400,256]{1,0:T(8,128)(2,1)S(1)} collective-permute-done((bf16[400,256]{1,0:T(8,128)(2,1)S(1)}, bf16[400,256]{1,0:T(8,128)(2,1)S(1)}, u32[]{:S(2)}, u32[]{:S(2)}) %collective-permute-start.8) | collective-permute-done | bytes 204832 | tf_op jit(solution)/shard_map/ppermute | solution.py:44
  19.6 1.5 %collective-permute-start.5 = (bf16[400,256]{1,0:T(8,128)(2,1)S(1)}, bf16[400,256]{1,0:T(8,128)(2,1)S(1)}, u32[]{:S(2)}, u32[]{:S(2)}) collective-permute-start(bf16[400,256]{1,0:T(8,128)(2,1)S(1)} %collective-permute-done.1.refs_2_), channel_id=1, source_target_pairs={{0,128},{8,136},{16,144},{24,152},{32,160},{40,168},{48,176},{56,1... | collective-permute-start | bytes 614408 | tf_op jit(solution)/shard_map/ppermute | solution.py:44
  21.1 0.0 collective-permute-done.10.refs_4_
  21.2 2.5 %collective-permute-start.13 = (bf16[192,256]{1,0:T(8,128)(2,1)S(1)}, bf16[192,256]{1,0:T(8,128)(2,1)S(1)}, u32[]{:S(2)}, u32[]{:S(2)}) collective-permute-start(bf16[192,256]{1,0:T(8,128)(2,1)S(1)} %slice.9), channel_id=1, source_target_pairs={{0,96},{8,104},{16,112},{24,120},{32,64},{40,72},{48,80},{56,88},{... | collective-permute-start | bytes 294920 | tf_op jit(solution)/shard_map/ppermute | solution.py:44
  23.7 3.4 %collective-permute-start.12 = (bf16[208,256]{1,0:T(8,128)(2,1)S(1)}, bf16[208,256]{1,0:T(8,128)(2,1)S(1)}, u32[]{:S(2)}, u32[]{:S(2)}) collective-permute-start(bf16[208,256]{1,0:T(8,128)(2,1)S(1)} %slice.8), channel_id=1, source_target_pairs={{0,32},{8,40},{16,48},{24,56},{32,0},{40,8},{48,16},{56,24},{64,96... | collective-permute-start | bytes 319496 | tf_op jit(solution)/shard_map/ppermute | solution.py:44
  27.1 0.5 collective-permute-start.9
  27.6 0.7 collective-permute-done.13.refs_5_
  28.4 0.5 collective-permute-start.6
  28.9 1.0 collective-permute-done.12.refs_4_
  29.8 0.1 pad_add_fusion.where_ref
  29.9 0.5 collective-permute-start.15
  30.4 0.3 collective-permute-start.14
  30.7 2.7 %shard_map.76 = (bf16[1536,128]{1,0:T(8,128)(2,1)S(1)}, bf16[1536,128]{1,0:T(8,128)(2,1)S(1)}, f32[8,1536]{1,0:T(8,128)S(1)}, bf16[768,128]{1,0:T(8,128)(2,1)S(1...) custom-call(s32[2]{0:T(128)S(1)} %pad_add_fusion.where_ref, ...), custom_call_target="tpu_custom_call" | custom-call | flops 2000000000 | bytes 4000000 | tf_op jit(solution)/shard_map/pallas_call | solution.py:243
  33.4 1.5 %shard_map.77 = (bf16[384,128]{1,0:T(8,128)(2,1)S(1)}, f32[384,1536]{1,0:T(8,128)S(1)}, f32[384,1536]{1,0:T(8,128)S(1)}, f32[3,8,1536]{2,1,0:T(8,128)S(1)}) custom-call(s32[2]{0:T(128)S(1)} %pad_add_fusion.where_ref, bf16[1536,128]{1,0:T(8,128)(2,1)S(1)} %get-tuple-element.26.refs_0_, bf16[1536,128]{1,0:T(8,128)(2,1)S(1)} %get-tuple-element.27.refs_1_, ...), custom_call_target="tpu_custom_call" | custom-call | flops 1000000000 | bytes 4000000 | tf_op jit(solution)/shard_map/pallas_call | solution.py:243
  35.0 1.6 %shard_map.78 = (bf16[384,128]{1,0:T(8,128)(2,1)S(1)}, f32[384,1536]{1,0:T(8,128)S(1)}, f32[384,1536]{1,0:T(8,128)S(1)}, f32[8,768]{1,0:T(8,128)S(1)}) custom-call(s32[2]{0:T(128)S(1)} %pad_add_fusion.where_ref, bf16[1536,128]{1,0:T(8,128)(2,1)S(1)} %get-tuple-element.26.refs_0_, bf16[1536,128]{1,0:T(8,128)(2,1)S(1)} %get-tuple-element.27.refs_1_, ...), custom_call_target="tpu_custom_call" | custom-call | flops 1000000000 | bytes 4000000 | tf_op jit(solution)/shard_map/pallas_call | solution.py:243
  36.6 2.7 %collective-permute-start.16 = (f32[8,768]{1,0:T(8,128)S(1)}, f32[8,768]{1,0:T(8,128)S(1)}, u32[]{:S(2)}, u32[]{:S(2)}) collective-permute-start(f32[8,768]{1,0:T(8,128)S(1)} %get-tuple-element.40.refs_11_), channel_id=1, source_target_pairs={{0,16},{8,24},{16,0},{24,8},{32,48},{40,56},{48,32},{56,40},{64,80... | collective-permute-start | bytes 73736 | tf_op jit(solution)/shard_map/ppermute | solution.py:44
  39.3 0.5 collective-permute-start.17
  39.8 1.0 %collective-permute-start.18 = (f32[8,768]{1,0:T(8,128)S(1)}, f32[8,768]{1,0:T(8,128)S(1)}, u32[]{:S(2)}, u32[]{:S(2)}) collective-permute-start(f32[8,768]{1,0:T(8,128)S(1)} %get-tuple-element.40.refs_11_), channel_id=1, source_target_pairs={{0,144},{8,152},{16,128},{24,136},{32,176},{40,184},{48,160},{56,1... | collective-permute-start | bytes 73736 | tf_op jit(solution)/shard_map/ppermute | solution.py:44
  40.8 0.2 collective-permute-done.16.refs_12_
  41.1 2.3 %collective-permute-done.17.refs_13_ = f32[8,768]{1,0:T(8,128)S(1)} collective-permute-done((f32[8,768]{1,0:T(8,128)S(1)}, f32[8,768]{1,0:T(8,128)S(1)}, u32[]{:S(2)}, u32[]{:S(2)}) %collective-permute-start.17) | collective-permute-done | bytes 24608 | tf_op jit(solution)/shard_map/ppermute | solution.py:44
  43.4 1.2 %collective-permute-done.18.refs_14_ = f32[8,768]{1,0:T(8,128)S(1)} collective-permute-done((f32[8,768]{1,0:T(8,128)S(1)}, f32[8,768]{1,0:T(8,128)S(1)}, u32[]{:S(2)}, u32[]{:S(2)}) %collective-permute-start.18) | collective-permute-done | bytes 24608 | tf_op jit(solution)/shard_map/ppermute | solution.py:44
  44.5 4.5 %shard_map.79 = (f32[384,128]{1,0:T(8,128)S(1)}, bf16[384,128]{1,0:T(8,128)(2,1)S(1)}, bf16[384,128]{1,0:T(8,128)(2,1)S(1)}, bf16[384,128]{1,0:T(8,128)(2,1)S(1)...) custom-call(s32[2]{0:T(128)S(1)} %pad_add_fusion.where_ref, ...), custom_call_target="tpu_custom_call" | custom-call | flops 6000000000 | bytes 4000000 | tf_op jit(solution)/shard_map/pallas_call | solution.py:243
  49.0 0.2 collective-permute-start.19
  49.2 1.5 %collective-permute-start.20 = (bf16[384,128]{1,0:T(8,128)(2,1)S(1)}, bf16[384,128]{1,0:T(8,128)(2,1)S(1)}, u32[]{:S(2)}, u32[]{:S(2)}) collective-permute-start(bf16[384,128]{1,0:T(8,128)(2,1)S(1)} %get-tuple-element.43), channel_id=1, source_target_pairs={{0,128},{8,136},{16,144},{24,152},{32,160},{40,168},{48,176},{56,1... | collective-permute-start | bytes 294920 | tf_op jit(solution)/shard_map/ppermute | solution.py:44
  50.7 1.9 %collective-permute-start.21 = (bf16[384,128]{1,0:T(8,128)(2,1)S(1)}, bf16[384,128]{1,0:T(8,128)(2,1)S(1)}, u32[]{:S(2)}, u32[]{:S(2)}) collective-permute-start(bf16[384,128]{1,0:T(8,128)(2,1)S(1)} %get-tuple-element.44), channel_id=1, source_target_pairs={{0,144},{8,152},{16,128},{24,136},{32,176},{40,184},{48,160},{56,1... | collective-permute-start | bytes 294920 | tf_op jit(solution)/shard_map/ppermute | solution.py:44
  52.6 1.1 %collective-permute-done.19 = bf16[384,128]{1,0:T(8,128)(2,1)S(1)} collective-permute-done((bf16[384,128]{1,0:T(8,128)(2,1)S(1)}, bf16[384,128]{1,0:T(8,128)(2,1)S(1)}, u32[]{:S(2)}, u32[]{:S(2)}) %collective-permute-start.19) | collective-permute-done | bytes 98336 | tf_op jit(solution)/shard_map/ppermute | solution.py:44
  53.7 0.8 collective-permute-done.20
  54.5 1.7 %collective-permute-done.21 = bf16[384,128]{1,0:T(8,128)(2,1)S(1)} collective-permute-done((bf16[384,128]{1,0:T(8,128)(2,1)S(1)}, bf16[384,128]{1,0:T(8,128)(2,1)S(1)}, u32[]{:S(2)}, u32[]{:S(2)}) %collective-permute-start.21) | collective-permute-done | bytes 98336 | tf_op jit(solution)/shard_map/ppermute | solution.py:44
  56.3 0.1 collective-permute-start.22
  56.4 2.6 %collective-permute-start.23 = (bf16[768,128]{1,0:T(8,128)(2,1)S(1)}, bf16[768,128]{1,0:T(8,128)(2,1)S(1)}, u32[]{:S(2)}, u32[]{:S(2)}) collective-permute-start(bf16[768,128]{1,0:T(8,128)(2,1)S(1)} %get-tuple-element.46), channel_id=1, source_target_pairs={{0,32},{8,40},{16,48},{24,56},{32,0},{40,8},{48,16},{56,24},{64,96... | collective-permute-start | bytes 589832 | tf_op jit(solution)/shard_map/ppermute | solution.py:44
  59.0 2.0 %collective-permute-start.24 = (bf16[768,128]{1,0:T(8,128)(2,1)S(1)}, bf16[768,128]{1,0:T(8,128)(2,1)S(1)}, u32[]{:S(2)}, u32[]{:S(2)}) collective-permute-start(bf16[768,128]{1,0:T(8,128)(2,1)S(1)} %get-tuple-element.47), channel_id=1, source_target_pairs={{0,96},{8,104},{16,112},{24,120},{32,64},{40,72},{48,80},{56,88},{... | collective-permute-start | bytes 589832 | tf_op jit(solution)/shard_map/ppermute | solution.py:44
  61.0 2.0 %collective-permute-start.25 = (bf16[768,128]{1,0:T(8,128)(2,1)S(1)}, bf16[768,128]{1,0:T(8,128)(2,1)S(1)}, u32[]{:S(2)}, u32[]{:S(2)}) collective-permute-start(bf16[768,128]{1,0:T(8,128)(2,1)S(1)} %get-tuple-element.48), channel_id=1, source_target_pairs={{0,64},{8,72},{16,80},{24,88},{32,96},{40,104},{48,112},{56,120},{... | collective-permute-start | bytes 589832 | tf_op jit(solution)/shard_map/ppermute | solution.py:44
  63.0 9.6 %collective-permute-done.23 = bf16[768,128]{1,0:T(8,128)(2,1)S(1)} collective-permute-done((bf16[768,128]{1,0:T(8,128)(2,1)S(1)}, bf16[768,128]{1,0:T(8,128)(2,1)S(1)}, u32[]{:S(2)}, u32[]{:S(2)}) %collective-permute-start.23) | collective-permute-done | bytes 196640 | tf_op jit(solution)/shard_map/ppermute | solution.py:44
  72.6 7.6 %collective-permute-done.24 = bf16[768,128]{1,0:T(8,128)(2,1)S(1)} collective-permute-done((bf16[768,128]{1,0:T(8,128)(2,1)S(1)}, bf16[768,128]{1,0:T(8,128)(2,1)S(1)}, u32[]{:S(2)}, u32[]{:S(2)}) %collective-permute-start.24) | collective-permute-done | bytes 196640 | tf_op jit(solution)/shard_map/ppermute | solution.py:44
  80.2 0.1 add_convert_fusion
  80.3 0.1 collective-permute-start.26
  80.5 14.7 %all_to_all.5 = bf16[8,24,256]{2,1,0:T(8,128)(2,1)S(1)} all-to-all(bf16[8,24,256]{2,1,0:T(8,128)(2,1)S(1)} %bitcast.28), channel_id=1, replica_groups=mesh['seq'=32,'head'=8] {'head'}, dimensions={0} | all-to-all | bytes 196608 | tf_op jit(solution)/shard_map/all_to_all | solution.py:313
  95.2 0.6 copy.9
  95.9 0.7 fusion.4
  (29 shorter events, 0.2 us)
Async XLA Ops:
  2.4 11.0 %collective-permute-start.1 = (bf16[400,256]{1,0:T(8,128)(2,1)S(1)}, bf16[400,256]{1,0:T(8,128)(2,1)S(1)}, u32[]{:S(2)}, u32[]{:S(2)}) collective-permute-start(bf16[400,256]{1,0:T(8,128)(2,1)S(1)} %get-tuple-element.56.refs_0_), channel_id=1, source_target_pairs={{0,16},{8,24},{16,0},{24,8},{32,48},{40,56},{48,32},{56,40},{64,80... | collective-permute-start | bytes 614408 | tf_op jit(solution)/shard_map/ppermute | solution.py:44
  4.3 15.3 %collective-permute-start.8 = (bf16[400,256]{1,0:T(8,128)(2,1)S(1)}, bf16[400,256]{1,0:T(8,128)(2,1)S(1)}, u32[]{:S(2)}, u32[]{:S(2)}) collective-permute-start(bf16[400,256]{1,0:T(8,128)(2,1)S(1)} %get-tuple-element.55.refs_8_), channel_id=1, source_target_pairs={{0,32},{8,40},{16,48},{24,56},{32,0},{40,8},{48,16},{56,24},{64,96... | collective-permute-start | bytes 614408 | tf_op jit(solution)/shard_map/ppermute | solution.py:44
  5.9 15.2 %collective-permute-start.10 = (bf16[400,256]{1,0:T(8,128)(2,1)S(1)}, bf16[400,256]{1,0:T(8,128)(2,1)S(1)}, u32[]{:S(2)}, u32[]{:S(2)}) collective-permute-start(bf16[400,256]{1,0:T(8,128)(2,1)S(1)} %get-tuple-element.55.refs_8_), channel_id=1, source_target_pairs={{0,96},{8,104},{16,112},{24,120},{32,64},{40,72},{48,80},{56,88},{... | collective-permute-start | bytes 614408 | tf_op jit(solution)/shard_map/ppermute | solution.py:44
  10.4 13.3 %collective-permute-start.3 = (bf16[400,256]{1,0:T(8,128)(2,1)S(1)}, bf16[400,256]{1,0:T(8,128)(2,1)S(1)}, u32[]{:S(2)}, u32[]{:S(2)}) collective-permute-start(bf16[400,256]{1,0:T(8,128)(2,1)S(1)} %get-tuple-element.56.refs_0_), channel_id=1, source_target_pairs={{0,128},{8,136},{16,144},{24,152},{32,160},{40,168},{48,176},{56,1... | collective-permute-start | bytes 614408 | tf_op jit(solution)/shard_map/ppermute | solution.py:44
  11.9 15.3 %collective-permute-start = (bf16[400,256]{1,0:T(8,128)(2,1)S(1)}, bf16[400,256]{1,0:T(8,128)(2,1)S(1)}, u32[]{:S(2)}, u32[]{:S(2)}) collective-permute-start(bf16[400,256]{1,0:T(8,128)(2,1)S(1)} %get-tuple-element.56.refs_0_), channel_id=1, source_target_pairs={{0,8},{8,0},{16,24},{24,16},{32,40},{40,32},{48,56},{56,48},{64,72... | collective-permute-start | bytes 614408 | tf_op jit(solution)/shard_map/ppermute | solution.py:44
  13.4 13.7 %collective-permute-start.7 = (bf16[400,256]{1,0:T(8,128)(2,1)S(1)}, bf16[400,256]{1,0:T(8,128)(2,1)S(1)}, u32[]{:S(2)}, u32[]{:S(2)}) collective-permute-start(bf16[400,256]{1,0:T(8,128)(2,1)S(1)} %get-tuple-element.55.refs_8_), channel_id=1, source_target_pairs={{0,8},{8,0},{16,24},{24,16},{32,40},{40,32},{48,56},{56,48},{64,72... | collective-permute-start | bytes 614408 | tf_op jit(solution)/shard_map/ppermute | solution.py:44
  19.6 8.7 %collective-permute-start.5 = (bf16[400,256]{1,0:T(8,128)(2,1)S(1)}, bf16[400,256]{1,0:T(8,128)(2,1)S(1)}, u32[]{:S(2)}, u32[]{:S(2)}) collective-permute-start(bf16[400,256]{1,0:T(8,128)(2,1)S(1)} %collective-permute-done.1.refs_2_), channel_id=1, source_target_pairs={{0,128},{8,136},{16,144},{24,152},{32,160},{40,168},{48,176},{56,1... | collective-permute-start | bytes 614408 | tf_op jit(solution)/shard_map/ppermute | solution.py:44
  21.2 7.2 %collective-permute-start.13 = (bf16[192,256]{1,0:T(8,128)(2,1)S(1)}, bf16[192,256]{1,0:T(8,128)(2,1)S(1)}, u32[]{:S(2)}, u32[]{:S(2)}) collective-permute-start(bf16[192,256]{1,0:T(8,128)(2,1)S(1)} %slice.9), channel_id=1, source_target_pairs={{0,96},{8,104},{16,112},{24,120},{32,64},{40,72},{48,80},{56,88},{... | collective-permute-start | bytes 294920 | tf_op jit(solution)/shard_map/ppermute | solution.py:44
  23.7 6.1 %collective-permute-start.12 = (bf16[208,256]{1,0:T(8,128)(2,1)S(1)}, bf16[208,256]{1,0:T(8,128)(2,1)S(1)}, u32[]{:S(2)}, u32[]{:S(2)}) collective-permute-start(bf16[208,256]{1,0:T(8,128)(2,1)S(1)} %slice.8), channel_id=1, source_target_pairs={{0,32},{8,40},{16,48},{24,56},{32,0},{40,8},{48,16},{56,24},{64,96... | collective-permute-start | bytes 319496 | tf_op jit(solution)/shard_map/ppermute | solution.py:44
  27.1 2.8 %collective-permute-start.2 = (bf16[400,256]{1,0:T(8,128)(2,1)S(1)}, bf16[400,256]{1,0:T(8,128)(2,1)S(1)}, u32[]{:S(2)}, u32[]{:S(2)}) collective-permute-start(bf16[400,256]{1,0:T(8,128)(2,1)S(1)} %collective-permute-done.1.refs_2_), channel_id=1, source_target_pairs={{0,8},{8,0},{16,24},{24,16},{32,40},{40,32},{48,56},{56,48},{64,72... | collective-permute-start | bytes 614408 | tf_op jit(solution)/shard_map/ppermute | solution.py:44
  27.1 3.3 %collective-permute-start.9 = (bf16[400,256]{1,0:T(8,128)(2,1)S(1)}, bf16[400,256]{1,0:T(8,128)(2,1)S(1)}, u32[]{:S(2)}, u32[]{:S(2)}) collective-permute-start(bf16[400,256]{1,0:T(8,128)(2,1)S(1)} %collective-permute-done.8.refs_10_), channel_id=1, source_target_pairs={{0,8},{8,0},{16,24},{24,16},{32,40},{40,32},{48,56},{56,48},{64,72... | collective-permute-start | bytes 614408 | tf_op jit(solution)/shard_map/ppermute | solution.py:44
  28.4 2.4 %collective-permute-start.4 = (bf16[400,256]{1,0:T(8,128)(2,1)S(1)}, bf16[400,256]{1,0:T(8,128)(2,1)S(1)}, u32[]{:S(2)}, u32[]{:S(2)}) collective-permute-start(bf16[400,256]{1,0:T(8,128)(2,1)S(1)} %collective-permute-done.3.refs_4_), channel_id=1, source_target_pairs={{0,8},{8,0},{16,24},{24,16},{32,40},{40,32},{48,56},{56,48},{64,72... | collective-permute-start | bytes 614408 | tf_op jit(solution)/shard_map/ppermute | solution.py:44
  28.4 2.4 %collective-permute-start.6 = (bf16[400,256]{1,0:T(8,128)(2,1)S(1)}, bf16[400,256]{1,0:T(8,128)(2,1)S(1)}, u32[]{:S(2)}, u32[]{:S(2)}) collective-permute-start(bf16[400,256]{1,0:T(8,128)(2,1)S(1)} %collective-permute-done.5.refs_6_), channel_id=1, source_target_pairs={{0,8},{8,0},{16,24},{24,16},{32,40},{40,32},{48,56},{56,48},{64,72... | collective-permute-start | bytes 614408 | tf_op jit(solution)/shard_map/ppermute | solution.py:44
  29.8 3.6 %collective-permute-start.11 = (bf16[400,256]{1,0:T(8,128)(2,1)S(1)}, bf16[400,256]{1,0:T(8,128)(2,1)S(1)}, u32[]{:S(2)}, u32[]{:S(2)}) collective-permute-start(bf16[400,256]{1,0:T(8,128)(2,1)S(1)} %collective-permute-done.10.refs_4_), channel_id=1, source_target_pairs={{0,8},{8,0},{16,24},{24,16},{32,40},{40,32},{48,56},{56,48},{64,72... | collective-permute-start | bytes 614408 | tf_op jit(solution)/shard_map/ppermute | solution.py:44
  29.9 5.1 %collective-permute-start.15 = (bf16[192,256]{1,0:T(8,128)(2,1)S(1)}, bf16[192,256]{1,0:T(8,128)(2,1)S(1)}, u32[]{:S(2)}, u32[]{:S(2)}) collective-permute-start(bf16[192,256]{1,0:T(8,128)(2,1)S(1)} %collective-permute-done.13.refs_5_), channel_id=1, source_target_pairs={{0,8},{8,0},{16,24},{24,16},{32,40},{40,32},{48,56},{56,48},{64,72... | collective-permute-start | bytes 294920 | tf_op jit(solution)/shard_map/ppermute | solution.py:44
  30.4 4.5 %collective-permute-start.14 = (bf16[208,256]{1,0:T(8,128)(2,1)S(1)}, bf16[208,256]{1,0:T(8,128)(2,1)S(1)}, u32[]{:S(2)}, u32[]{:S(2)}) collective-permute-start(bf16[208,256]{1,0:T(8,128)(2,1)S(1)} %collective-permute-done.12.refs_4_), channel_id=1, source_target_pairs={{0,8},{8,0},{16,24},{24,16},{32,40},{40,32},{48,56},{56,48},{64,72... | collective-permute-start | bytes 319496 | tf_op jit(solution)/shard_map/ppermute | solution.py:44
  36.6 4.5 %collective-permute-start.16 = (f32[8,768]{1,0:T(8,128)S(1)}, f32[8,768]{1,0:T(8,128)S(1)}, u32[]{:S(2)}, u32[]{:S(2)}) collective-permute-start(f32[8,768]{1,0:T(8,128)S(1)} %get-tuple-element.40.refs_11_), channel_id=1, source_target_pairs={{0,16},{8,24},{16,0},{24,8},{32,48},{40,56},{48,32},{56,40},{64,80... | collective-permute-start | bytes 73736 | tf_op jit(solution)/shard_map/ppermute | solution.py:44
  39.3 4.1 %collective-permute-start.17 = (f32[8,768]{1,0:T(8,128)S(1)}, f32[8,768]{1,0:T(8,128)S(1)}, u32[]{:S(2)}, u32[]{:S(2)}) collective-permute-start(f32[8,768]{1,0:T(8,128)S(1)} %get-tuple-element.40.refs_11_), channel_id=1, source_target_pairs={{0,128},{8,136},{16,144},{24,152},{32,160},{40,168},{48,176},{56,1... | collective-permute-start | bytes 73736 | tf_op jit(solution)/shard_map/ppermute | solution.py:44
  39.8 4.7 %collective-permute-start.18 = (f32[8,768]{1,0:T(8,128)S(1)}, f32[8,768]{1,0:T(8,128)S(1)}, u32[]{:S(2)}, u32[]{:S(2)}) collective-permute-start(f32[8,768]{1,0:T(8,128)S(1)} %get-tuple-element.40.refs_11_), channel_id=1, source_target_pairs={{0,144},{8,152},{16,128},{24,136},{32,176},{40,184},{48,160},{56,1... | collective-permute-start | bytes 73736 | tf_op jit(solution)/shard_map/ppermute | solution.py:44
  49.0 4.7 %collective-permute-start.19 = (bf16[384,128]{1,0:T(8,128)(2,1)S(1)}, bf16[384,128]{1,0:T(8,128)(2,1)S(1)}, u32[]{:S(2)}, u32[]{:S(2)}) collective-permute-start(bf16[384,128]{1,0:T(8,128)(2,1)S(1)} %get-tuple-element.42), channel_id=1, source_target_pairs={{0,16},{8,24},{16,0},{24,8},{32,48},{40,56},{48,32},{56,40},{64,80... | collective-permute-start | bytes 294920 | tf_op jit(solution)/shard_map/ppermute | solution.py:44
  49.2 5.3 %collective-permute-start.20 = (bf16[384,128]{1,0:T(8,128)(2,1)S(1)}, bf16[384,128]{1,0:T(8,128)(2,1)S(1)}, u32[]{:S(2)}, u32[]{:S(2)}) collective-permute-start(bf16[384,128]{1,0:T(8,128)(2,1)S(1)} %get-tuple-element.43), channel_id=1, source_target_pairs={{0,128},{8,136},{16,144},{24,152},{32,160},{40,168},{48,176},{56,1... | collective-permute-start | bytes 294920 | tf_op jit(solution)/shard_map/ppermute | solution.py:44
  50.7 5.5 %collective-permute-start.21 = (bf16[384,128]{1,0:T(8,128)(2,1)S(1)}, bf16[384,128]{1,0:T(8,128)(2,1)S(1)}, u32[]{:S(2)}, u32[]{:S(2)}) collective-permute-start(bf16[384,128]{1,0:T(8,128)(2,1)S(1)} %get-tuple-element.44), channel_id=1, source_target_pairs={{0,144},{8,152},{16,128},{24,136},{32,176},{40,184},{48,160},{56,1... | collective-permute-start | bytes 294920 | tf_op jit(solution)/shard_map/ppermute | solution.py:44
  56.3 6.7 %collective-permute-start.22 = (bf16[192,128]{1,0:T(8,128)(2,1)S(1)}, bf16[192,128]{1,0:T(8,128)(2,1)S(1)}, u32[]{:S(2)}, u32[]{:S(2)}) collective-permute-start(bf16[192,128]{1,0:T(8,128)(2,1)S(1)} %dynamic-slice_bitcast_fusion.1), channel_id=1, source_target_pairs={{0,8},{8,0},{16,24},{24,16},{32,40},{40,32},{48,56},{56,48},{64,72... | collective-permute-start | bytes 147464 | tf_op jit(solution)/shard_map/ppermute | solution.py:44
  56.4 16.2 %collective-permute-start.23 = (bf16[768,128]{1,0:T(8,128)(2,1)S(1)}, bf16[768,128]{1,0:T(8,128)(2,1)S(1)}, u32[]{:S(2)}, u32[]{:S(2)}) collective-permute-start(bf16[768,128]{1,0:T(8,128)(2,1)S(1)} %get-tuple-element.46), channel_id=1, source_target_pairs={{0,32},{8,40},{16,48},{24,56},{32,0},{40,8},{48,16},{56,24},{64,96... | collective-permute-start | bytes 589832 | tf_op jit(solution)/shard_map/ppermute | solution.py:44
  59.0 21.2 %collective-permute-start.24 = (bf16[768,128]{1,0:T(8,128)(2,1)S(1)}, bf16[768,128]{1,0:T(8,128)(2,1)S(1)}, u32[]{:S(2)}, u32[]{:S(2)}) collective-permute-start(bf16[768,128]{1,0:T(8,128)(2,1)S(1)} %get-tuple-element.47), channel_id=1, source_target_pairs={{0,96},{8,104},{16,112},{24,120},{32,64},{40,72},{48,80},{56,88},{... | collective-permute-start | bytes 589832 | tf_op jit(solution)/shard_map/ppermute | solution.py:44
  61.0 19.2 %collective-permute-start.25 = (bf16[768,128]{1,0:T(8,128)(2,1)S(1)}, bf16[768,128]{1,0:T(8,128)(2,1)S(1)}, u32[]{:S(2)}, u32[]{:S(2)}) collective-permute-start(bf16[768,128]{1,0:T(8,128)(2,1)S(1)} %get-tuple-element.48), channel_id=1, source_target_pairs={{0,64},{8,72},{16,80},{24,88},{32,96},{40,104},{48,112},{56,120},{... | collective-permute-start | bytes 589832 | tf_op jit(solution)/shard_map/ppermute | solution.py:44
  80.3 15.5 %collective-permute-start.26 = (bf16[2,192,128]{2,1,0:T(8,128)(2,1)S(1)}, bf16[2,192,128]{2,1,0:T(8,128)(2,1)S(1)}, u32[]{:S(2)}, u32[]{:S(2)}) collective-permute-start(bf16[2,192,128]{2,1,0:T(8,128)(2,1)S(1)} %dynamic-slice_bitcast_fusion), channel_id=1, source_target_pairs={{0,8},{8,0},{16,24},{24,16},{32,40},{40,32},{48,56},{56,48},{64,72... | collective-permute-start | bytes 294920 | tf_op jit(solution)/shard_map/ppermute | solution.py:44
